TPU v7x, 32 devices: a whole 2x2x4 slice. The times are simulated.
32 devices in a mesh: groups: 2 (over x), seq: 8 (over z, y), batch: 2 (over core).
Axes of the slice: x: 2, y: 2, z: 4, core: 2. Of those that a mesh axis runs over, the one named last changes fastest.
Arguments:
- prompt_cache: bfloat16 [16, 256, 8, 256], P(('groups', 'batch'), 'seq'), parts along dimension 0, may hold values from -6 to 6
- prompt_states: float32 [16, 8, 16, 16384], P(('groups', 'batch'), 'seq'), parts along dimension 0, may hold values from -6 to 6
- block_steps: float32 [16, 8, 16384], P(('groups', 'batch'), 'seq'), parts along dimension 0, may hold values from 0.005 to 0.1
- prompt_lengths: int32 [16], P('groups'), parts along dimension 0, may hold values from 42 to 255
- target_slots: int32 [16], P('groups'), parts along dimension 0, may hold values from 0 to 15, as said below
- cache_lengths: int32 [32], P(('groups', 'batch')), parts along dimension 0, may hold values from 42 to 255
- resident_cache: bfloat16 [32, 32, 8, 8, 256], P(('groups', 'batch'), None, 'seq'), parts along dimension 0, may hold values from -6 to 6
- token_cache: bfloat16 [32, 8, 256], P(('groups', 'batch')), parts along dimension 0, may hold values from -6 to 6
- queries: bfloat16 [32, 64, 128], P(('groups', 'batch')), parts along dimension 0, may hold values from -6 to 6
- resident_states: float32 [32, 16, 16384], P(('groups', 'batch'), None, 'seq'), parts along dimension 0, may hold values from -6 to 6
- decay_rates: float32 [16, 16384], replicated, may hold values from 0.05 to 10
- step_sizes: float32 [32, 16384], P(('groups', 'batch'), 'seq'), parts along dimension 0, may hold values from 0.01 to 1
- inner_input: bfloat16 [32, 16384], P(('groups', 'batch'), 'seq'), parts along dimension 0, may hold values from -6 to 6
- inner_gate: bfloat16 [32, 16384], P(('groups', 'batch'), 'seq'), parts along dimension 0, may hold values from -6 to 6
- state_input: float32 [32, 16], P(('groups', 'batch')), parts along dimension 0, may hold values from -6 to 6
- state_readout: float32 [32, 16], P(('groups', 'batch')), parts along dimension 0, may hold values from -6 to 6
- skip_gain: float32 [16384], P('seq'), may hold values from 0.5 to 1.5
Outputs:
- merged_cache: bfloat16 [32, 32, 8, 8, 256], P(('groups', 'batch'), None, 'seq'), parts along dimension 0
- attention: bfloat16 [32, 64, 128], P(('groups', 'batch'), 'seq'), parts along dimension 0
- next_states: float32 [32, 16, 16384], P(('groups', 'batch'), None, 'seq'), parts along dimension 0
- mamba_output: bfloat16 [32, 16384], P(('groups', 'batch'), 'seq'), parts along dimension 0
There are 2 independent parts, one for each index of `groups`. A program takes and returns all parts, laid end to end along the dimension named above; an argument that names none is the same for every part. Nothing has to cross between parts.
Inputs may be any that keep to these rules, and one draw needn't show every extreme that they name: `target_slots`: 8 distinct slots.
All inputs are finite; a program needn't handle non-finite values.
Results may differ from a plain program's by a relative error of at most 0.0019.
Values may be sent and summed in bfloat16 or wider, within the bound.
A program may use at most 320 MiB of HBM per device.

v0:
```python
import functools
import math

import jax
import jax.numpy as jnp
from jax import lax
from jax.experimental import pallas as pl
from jax.experimental.pallas import tpu as pltpu
from jax.sharding import PartitionSpec as P

MESH = pl.DeviceIdType.MESH
FULL = 32760.0
LOW = -1e30


def kernel(
    dims,
    plen,
    tslot,
    clen,
    cache_hbm,
    states_hbm,
    steps_hbm,
    resident_hbm,
    token_hbm,
    queries_hbm,
    rstates_hbm,
    rates_hbm,
    dt_hbm,
    inner_hbm,
    gate_hbm,
    s_in_hbm,
    s_out_hbm,
    skip_hbm,
    merged,
    attention,
    nstates,
    mout,
    arrived,
    cache_send,
    handed,
    acc,
    osend,
    orecv,
    lse_send,
    lse_recv,
    *rest,
):
    n, nb, levels, block_len = dims
    (
        cache,
        states,
        steps,
        resident,
        token,
        queries,
        rstates,
        rates,
        dt,
        inner,
        gate,
        s_in,
        s_out,
        skip,
        load_sems,
    ) = rest[:15]
    rest = rest[15:]
    hbm = (
        cache_hbm,
        states_hbm,
        steps_hbm,
        resident_hbm,
        token_hbm,
        queries_hbm,
        rstates_hbm,
        rates_hbm,
        dt_hbm,
        inner_hbm,
        gate_hbm,
        s_in_hbm,
        s_out_hbm,
        skip_hbm,
    )
    held = (
        cache,
        states,
        steps,
        resident,
        token,
        queries,
        rstates,
        rates,
        dt,
        inner,
        gate,
        s_in,
        s_out,
        skip,
    )
    d_send, d_recv, d_sel, d_cur, q_send, q_recv, m_send, m_recv = (
        rest[i * levels : (i + 1) * levels] for i in range(8)
    )
    (
        cache_ss, cache_rs, relay_ss, relay_rs, d_ss, d_rs, q_ss, q_rs, m_ss, m_rs,
        hand_ss, hand_rs, o_ss, o_rs, l_ss, l_rs,
    ) = rest[8 * levels :]
    me = lax.axis_index("seq")
    b = lax.axis_index("batch")
    prompts, rows, _, kv_heads, width = cache.shape
    all_prompts = prompts * nb
    requests, heads, head_dim = queries.shape
    state_n, channels = rates.shape
    share_len = channels // n
    chunk = min(512, share_len)
    per_share = share_len // chunk
    own_heads = heads // n
    group = heads // kv_heads
    positions = resident.shape[1]
    bits = [lax.rem(me // (1 << s), 2) for s in range(levels)]
    peers = [me + (1 - 2 * bits[s]) * (1 << s) for s in range(levels)]
    first = b * prompts

    def remote(src, dst, ss, rs, where):
        return pltpu.make_async_remote_copy(
            src_ref=src, dst_ref=dst, send_sem=ss, recv_sem=rs, device_id=where, device_id_type=MESH
        )

    loads = {}
    for i in (2, 0):
        loads[i] = pltpu.make_async_copy(hbm[i], held[i], load_sems.at[i])
        loads[i].start()
    for p in range(prompts):
        loads[1, p] = pltpu.make_async_copy(states_hbm.at[p], states.at[p], load_sems.at[14 + p])
        loads[1, p].start()
    for i in (3, 4, 5, 7, 6, 8, 9, 10, 11, 12, 13):
        loads[i] = pltpu.make_async_copy(hbm[i], held[i], load_sems.at[i])
        loads[i].start()

    barrier = pltpu.get_barrier_semaphore()
    for k in range(1, n):
        pl.semaphore_signal(
            barrier, inc=1, device_id={"seq": lax.rem(me + k, n)}, device_id_type=MESH
        )
    for k in range(1, nb):
        pl.semaphore_signal(
            barrier, inc=1, device_id={"batch": lax.rem(b + k, nb)}, device_id_type=MESH
        )
    pl.semaphore_wait(barrier, n - 1 + nb - 1)

    usable = [
        jnp.where(me * block_len < plen[first + p], 1.0, 0.0).astype(jnp.float32)
        for p in range(prompts)
    ]
    row_id = lax.broadcasted_iota(jnp.int32, (prompts, share_len), 0)
    usable_rows = jnp.zeros((prompts, share_len), jnp.float32)
    for p in range(prompts):
        usable_rows = jnp.where(row_id == p, usable[p], usable_rows)

    def lanes(share, c=0, size=share_len):
        return pl.ds(pl.multiple_of(share * share_len + c * chunk, 128), size)

    pending = []

    def start(copy):
        copy.start()
        pending.append(copy)
        return copy

    def steps_of(share):
        parts = [steps[p, :, lanes(share)] for p in range(prompts)]
        return jnp.concatenate(parts, axis=0) * usable_rows

    loads[2].wait()

    @pl.loop(0, n // 2)
    def _(k):
        d_send[0][k] = steps_of(2 * k + 1 - bits[0])

    d_copies = [
        remote(
            d_send[s].at[pl.ds(0, n >> (s + 1))],
            d_recv[s].at[pl.ds(0, n >> (s + 1))],
            d_ss.at[s],
            d_rs.at[s],
            {"seq": peers[s]},
        )
        for s in range(levels)
    ]
    start(d_copies[0])

    loads[0].wait()

    @pl.loop(0, n)
    def _(to):
        cache_send[to] = cache[:, :, to]

    cache_copies = []
    for k in range(1, n):
        to = lax.rem(me + k, n)
        cache_copies.append(
            start(
                remote(
                    cache_send.at[to],
                    arrived.at[b, me],
                    cache_ss.at[k - 1],
                    cache_rs.at[k - 1],
                    {"seq": to},
                )
            )
        )
    arrived[b, me] = cache[:, :, me]

    def read(s, p, k, c):
        if s == 0:
            share = k
            return states[p, :, lanes(share, c, chunk)] * usable[p]
        return acc[p, k, :, pl.ds(pl.multiple_of(c * chunk, 128), chunk)]

    q_copies, m_copies = {}, {}

    def send_half(s, p):
        count = (n >> (s + 1)) * per_share

        def largest(i, top):
            k, c = i // per_share, lax.rem(i, per_share)
            return jnp.maximum(top, jnp.abs(read(s, p, 2 * k + 1 - bits[s], c)))

        top = lax.fori_loop(0, count, largest, jnp.full((state_n, chunk), 1e-30, jnp.float32))
        top = jnp.max(jnp.max(top, axis=0, keepdims=True), axis=1, keepdims=True)
        m_send[s][p] = jnp.broadcast_to(top, (8, 128))
        scale = FULL / top

        @pl.loop(0, count)
        def _(i):
            k, c = i // per_share, lax.rem(i, per_share)
            value = read(s, p, 2 * k + 1 - bits[s], c) * scale
            q_send[s][p, k, :, pl.ds(pl.multiple_of(c * chunk, 128), chunk)] = (
                jnp.round(value).astype(jnp.int32).astype(jnp.int16)
            )

        where = {"seq": peers[s]}
        m_copies[s, p] = start(
            remote(m_send[s].at[p], m_recv[s].at[p], m_ss.at[s, p], m_rs.at[s, p], where)
        )
        q_copies[s, p] = start(
            remote(q_send[s].at[p], q_recv[s].at[p], q_ss.at[s, p], q_rs.at[s, p], where)
        )

    for p in range(prompts):
        loads[1, p].wait()
        send_half(0, p)

    def fold_steps(s):
        d_copies[s].wait_recv()
        right = jnp.full((prompts, share_len), bits[s], jnp.int32) == 1

        @pl.loop(0, n >> (s + 1))
        def _(k):
            if s == 0:
                own = steps_of(2 * k + bits[0])
            else:
                own = d_cur[s - 1][2 * k + bits[s]]
            other = d_recv[s][k]
            d_sel[s][k] = jnp.where(right, own, other)
            d_cur[s][k] = own + other

        if s + 1 < levels:

            @pl.loop(0, n >> (s + 2))
            def _(k):
                d_send[s + 1][k] = d_cur[s][2 * k + 1 - bits[s + 1]]

            start(d_copies[s + 1])

    fold_steps(0)

    for copy in cache_copies:
        copy.wait_recv()
    relays = []
    for k in range(1, nb):
        relays.append(
            start(
                remote(
                    arrived.at[b],
                    arrived.at[b],
                    relay_ss.at[k - 1],
                    relay_rs.at[k - 1],
                    {"batch": lax.rem(b + k, nb)},
                )
            )
        )
    for copy in relays:
        copy.wait_recv()

    def pick(r):
        slot = b * requests + r
        chosen, length, hits = jnp.int32(0), jnp.int32(0), jnp.int32(0)
        for p in range(all_prompts):
            hit = tslot[p] == slot
            chosen = jnp.where(hit, p, chosen)
            length = jnp.where(hit, plen[p], length)
            hits = jnp.where(hit, 1, hits)
        return chosen, hits, jnp.where(hits > 0, length, clen[r])

    shape3 = (positions, kv_heads, width)
    position = lax.broadcasted_iota(jnp.int32, shape3, 0) * n + me
    flat = positions * kv_heads
    column = lax.broadcasted_iota(jnp.int32, (heads, flat), 1)
    owner = lax.broadcasted_iota(jnp.int32, (heads, flat), 0) // group
    same_head = lax.rem(column, kv_heads) == owner
    column_position = (column // kv_heads) * n + me
    lane_id = lax.broadcasted_iota(jnp.int32, (heads, 128), 1)

    def attend(r, lse_all):
        chosen, hits, length = pick(r)
        fresh_limit = jnp.where(hits > 0, length, 0)
        new = arrived[chosen // prompts, :, lax.rem(chosen, prompts)].reshape(shape3).astype(jnp.float32)
        old = resident[r].astype(jnp.float32)
        x = jnp.where(position < fresh_limit, new, old)
        x = jnp.where(position < length, x, 0.0)
        x = jnp.where(position == length, token[r].astype(jnp.float32)[None], x)
        merged[r] = x.astype(jnp.bfloat16)
        x2 = x.reshape(flat, width)
        keys = x2[:, :head_dim].astype(jnp.bfloat16)
        values = x2[:, head_dim:].astype(jnp.bfloat16)
        score = lax.dot_general(
            queries[r], keys, (((1,), (1,)), ((), ())), preferred_element_type=jnp.float32
        ) * (1.0 / math.sqrt(head_dim))
        seen = same_head & (column_position <= length)
        score = jnp.where(seen, score, LOW)
        top = jnp.max(score, axis=1, keepdims=True)
        weight = jnp.where(seen, jnp.exp(score - top), 0.0)
        total = jnp.sum(weight, axis=1, keepdims=True)
        out = jnp.dot(weight.astype(jnp.bfloat16), values, preferred_element_type=jnp.float32)
        some = total > 0.0
        safe = jnp.where(some, total, 1.0)
        out = out / safe
        lse = jnp.where(some, top + jnp.log(safe), LOW)
        for j in range(n):
            osend[j, r] = out[j * own_heads : (j + 1) * own_heads]
        return jnp.where(lane_id == r, lse, lse_all)

    for s in range(1, levels):
        fold_steps(s)

    for i in (7, 6, 8, 9, 10, 11, 12, 13):
        loads[i].wait()
    hand_copies = []

    def fold(s, p):
        m_copies[s, p].wait_recv()
        q_copies[s, p].wait_recv()
        scale = m_recv[s][p][0:1, 0:1] * (1.0 / FULL)
        right = jnp.full((state_n, chunk), bits[s], jnp.int32) == 1
        below = lax.rem(me, 1 << (s + 1))

        @pl.loop(0, (n >> (s + 1)) * per_share)
        def _(i):
            k, c = i // per_share, lax.rem(i, per_share)
            at = pl.ds(pl.multiple_of(c * chunk, 128), chunk)
            other = q_recv[s][p, k, :, at].astype(jnp.int32).astype(jnp.float32) * scale
            own = read(s, p, 2 * k + bits[s], c)
            rate = rates[:, lanes(k * (1 << (s + 1)) + below, c, chunk)]
            decay = jnp.exp(-rate * d_sel[s][k, :, at][p : p + 1])
            early = jnp.where(right, other, own)
            late = jnp.where(right, own, other)
            folded = decay * early + late
            if s + 1 < levels:
                acc[p, k, :, at] = folded
            else:
                handed[first + p, :, at] = folded

        if s + 1 < levels:
            send_half(s + 1, p)
        else:
            for k in range(1, nb):
                hand_copies.append(
                    start(
                        remote(
                            handed.at[first + p],
                            handed.at[first + p],
                            hand_ss.at[k - 1, p],
                            hand_rs.at[k - 1, p],
                            {"batch": lax.rem(b + k, nb)},
                        )
                    )
                )

    o_copies = []

    def attention_part():
        for i in (3, 4, 5):
            loads[i].wait()
        lse_all = lax.fori_loop(0, requests, attend, jnp.zeros((heads, 128), jnp.float32))
        for j in range(n):
            lse_send[j] = lse_all[j * own_heads : (j + 1) * own_heads]
        for k in range(1, n):
            to = lax.rem(me + k, n)
            o_copies.append(
                start(
                    remote(
                        lse_send.at[to], lse_recv.at[me], l_ss.at[k - 1], l_rs.at[k - 1], {"seq": to}
                    )
                )
            )
            o_copies.append(
                start(
                    remote(osend.at[to], orecv.at[me], o_ss.at[k - 1], o_rs.at[k - 1], {"seq": to})
                )
            )
        lse_recv[me] = lse_send[me]
        orecv[me] = osend[me]

    for wave in range(prompts + levels - 1):
        if wave == levels - 1:
            attention_part()
        for s in reversed(range(levels)):
            p = wave - s
            if 0 <= p < prompts:
                fold(s, p)

    for copy in o_copies:
        copy.wait_recv()
    lane3 = lax.broadcasted_iota(jnp.int32, (n, own_heads, 128), 2)
    for r in range(requests):
        lse = jnp.sum(jnp.where(lane3 == r, lse_recv[...], 0.0), axis=2, keepdims=True)
        share = jnp.exp(lse - jnp.max(lse, axis=0, keepdims=True))
        top = jnp.sum(share * orecv[:, r], axis=0)
        attention[r] = (top / jnp.sum(share, axis=0)).astype(jnp.bfloat16)

    for copy in hand_copies:
        copy.wait_recv()

    eye = lax.broadcasted_iota(jnp.int32, (state_n, state_n), 0) == lax.broadcasted_iota(
        jnp.int32, (state_n, state_n), 1
    )

    def as_column(row):
        spread = jnp.where(eye, jnp.broadcast_to(row, (state_n, state_n)), 0.0)
        return jnp.sum(spread, axis=1, keepdims=True)

    picks = [pick(r) for r in range(requests)]
    in_all, out_all = s_in[...], s_out[...]
    in_cols = [as_column(in_all[r : r + 1]) for r in range(requests)]
    out_cols = [as_column(out_all[r : r + 1]) for r in range(requests)]

    @pl.loop(0, per_share)
    def _(c):
        at = pl.ds(pl.multiple_of(c * chunk, 128), chunk)
        step_rows = dt[:, at]
        x_rows = inner[:, at].astype(jnp.float32)
        g = gate[:, at].astype(jnp.float32)
        rate = -rates[:, lanes(me, c, chunk)]
        push_rows = step_rows * x_rows
        out_rows = []
        for r in range(requests):
            chosen, hits, _ = picks[r]
            fresh = jnp.full((state_n, chunk), hits, jnp.int32) > 0
            begin = jnp.where(fresh, handed[chosen, :, at], rstates[r, :, at])
            after = jnp.exp(rate * step_rows[r : r + 1]) * begin
            after = after + push_rows[r : r + 1] * in_cols[r]
            nstates[r, :, at] = after
            out_rows.append(jnp.sum(out_cols[r] * after, axis=0, keepdims=True))
        read_out = jnp.concatenate(out_rows, axis=0) + skip[:, at] * x_rows
        mout[:, at] = (read_out * (g / (1.0 + jnp.exp(-g)))).astype(jnp.bfloat16)

    for copy in pending:
        copy.wait_send()


def local(
    n,
    nb,
    prompt_cache,
    prompt_states,
    block_steps,
    prompt_lengths,
    target_slots,
    cache_lengths,
    resident_cache,
    token_cache,
    queries,
    resident_states,
    decay_rates,
    step_sizes,
    inner_input,
    inner_gate,
    state_input,
    state_readout,
    skip_gain,
):
    levels = n.bit_length() - 1
    prompts, block_len, kv_heads, width = prompt_cache.shape
    requests, heads, head_dim = queries.shape
    state_n, channels = decay_rates.shape
    share = channels // n
    own_heads = heads // n
    positions = resident_cache.shape[1]
    all_prompts = prompts * nb
    f32, bf16, i16 = jnp.float32, jnp.bfloat16, jnp.int16
    vmem = pl.BlockSpec(memory_space=pltpu.VMEM)
    smem = pl.BlockSpec(memory_space=pltpu.SMEM)
    dma = pltpu.SemaphoreType.DMA
    halves = [n >> (s + 1) for s in range(levels)]
    operands = (
        prompt_cache.reshape(prompts, block_len // n, n, kv_heads, width),
        prompt_states[:, 0],
        block_steps,
        resident_cache[:, :, 0],
        token_cache,
        queries,
        resident_states,
        decay_rates,
        step_sizes,
        inner_input,
        inner_gate,
        state_input,
        state_readout,
        skip_gain[None],
    )
    scratch = [
        pltpu.VMEM((nb, n, prompts, block_len // n, kv_heads, width), bf16),
        pltpu.VMEM((n, prompts, block_len // n, kv_heads, width), bf16),
        pltpu.VMEM((all_prompts, state_n, share), f32),
        pltpu.VMEM((prompts, n // 2, state_n, share), f32),
        pltpu.VMEM((n, requests, own_heads, head_dim), f32),
        pltpu.VMEM((n, requests, own_heads, head_dim), f32),
        pltpu.VMEM((n, own_heads, 128), f32),
        pltpu.VMEM((n, own_heads, 128), f32),
    ]
    scratch += [pltpu.VMEM(x.shape, x.dtype) for x in operands]
    scratch += [dma((len(operands) + prompts,))]
    for _ in range(4):
        scratch += [pltpu.VMEM((h + 1, prompts, share), f32) for h in halves]
    for _ in range(2):
        scratch += [pltpu.VMEM((prompts, h, state_n, share), i16) for h in halves]
    for _ in range(2):
        scratch += [pltpu.VMEM((prompts, 8, 128), f32) for h in halves]
    scratch += [dma((n - 1,))] * 2
    scratch += [dma((max(nb - 1, 1),))] * 2
    scratch += [dma((levels,))] * 2
    scratch += [dma((levels, prompts))] * 4
    scratch += [dma((max(nb - 1, 1), prompts))] * 2
    scratch += [dma((n - 1,))] * 4
    merged, attention, next_states, mamba_output = pl.pallas_call(
        functools.partial(kernel, (n, nb, levels, block_len)),
        out_shape=(
            jax.ShapeDtypeStruct((requests, positions, kv_heads, width), bf16),
            jax.ShapeDtypeStruct((requests, own_heads, head_dim), bf16),
            jax.ShapeDtypeStruct((requests, state_n, share), f32),
            jax.ShapeDtypeStruct((requests, share), bf16),
        ),
        in_specs=[smem] * 3 + [pl.BlockSpec(memory_space=pltpu.HBM)] * 14,
        out_specs=(vmem,) * 4,
        scratch_shapes=scratch,
        compiler_params=pltpu.CompilerParams(
            collective_id=0, has_side_effects=True, vmem_limit_bytes=67043328
        ),
    )(
        prompt_lengths,
        target_slots,
        cache_lengths,
        *operands,
    )
    return merged[:, :, None], attention, next_states, mamba_output


def solution(mesh):
    n, nb = mesh.shape["seq"], mesh.shape["batch"]
    return jax.shard_map(
        functools.partial(local, n, nb),
        mesh=mesh,
        in_specs=(
            P(("groups", "batch"), "seq", None, None),
            P(("groups", "batch"), "seq", None, None),
            P(("groups", "batch"), "seq", None),
            P("groups"),
            P("groups"),
            P(("groups", "batch")),
            P(("groups", "batch"), None, "seq", None, None),
            P(("groups", "batch"), None, None),
            P(("groups", "batch"), None, None),
            P(("groups", "batch"), None, "seq"),
            P(),
            P(("groups", "batch"), "seq"),
            P(("groups", "batch"), "seq"),
            P(("groups", "batch"), "seq"),
            P(("groups", "batch"), None),
            P(("groups", "batch"), None),
            P("seq"),
        ),
        out_specs=(
            P(("groups", "batch"), None, "seq", None, None),
            P(("groups", "batch"), "seq", None),
            P(("groups", "batch"), None, "seq"),
            P(("groups", "batch"), "seq"),
        ),
        check_vma=False,
    )
```

profile of v0, /device:TPU:0, one launch (start us, length us, event | category | flops | bytes accessed | tf_op | source)
XLA Modules:
  0.0 66.5 jit_solution(15946417980420548712)
XLA Ops:
  0.6 59.4 %shard_map.192 = (bf16[8,32,8,256]{3,2,1,0:T(8,128)(2,1)}, bf16[8,8,128]{2,1,0:T(8,128)(2,1)}, f32[8,16,2048]{2,1,0:T(8,128)}, bf16[8,2048]{1,0:T(8,128)(2,1)}) custom-call(s32[8]{0:T(128)} %plen.1, s32[8]{0:T(128)} %tslot.1, s32[8]{0:T(128)} %clen.1, bf16[4,4,8,8,256]{4,3,2,1,0:T(8,128)(2,1)} %bitcast.10, f32[4,16,16384]{2,1,0:T(8,128)} %bitcast.7, ...), custom_call_target="tpu_custom_call" | custom-call | tf_op jit(solution)/shard_map/pallas_call | solution.py:545
  60.0 0.0 copy-start
  60.0 2.3 %copy.26 = bf16[8,32,1,8,256]{4,3,2,1,0:T(8,128)(2,1)} copy(bf16[8,32,1,8,256]{4,3,2,1,0:T(8,128)(2,1)} %bitcast.9) | data formatting | bytes 2097152
  62.3 1.3 %copy.27 = bf16[8,8,128]{2,1,0:T(8,128)(2,1)} copy(bf16[8,8,128]{2,1,0:T(8,128)(2,1)} %get-tuple-element.21) | data formatting | bytes 32768
  63.6 2.3 %copy.28 = f32[8,16,2048]{2,1,0:T(8,128)} copy(f32[8,16,2048]{2,1,0:T(8,128)} %get-tuple-element.22) | data formatting | bytes 2097152
  65.9 0.0 copy-done
  65.9 0.6 copy.29
Async XLA Ops:
  60.0 5.9 %copy-start = (bf16[8,2048]{1,0:T(8,128)(2,1)S(1)}, bf16[8,2048]{1,0:T(8,128)(2,1)}, u32[]{:S(2)}) copy-start(bf16[8,2048]{1,0:T(8,128)(2,1)} %get-tuple-element.23) | copy-start | bytes 98308
where the time goes:
time: 67.5 us; the launch traced here: 66.5 us
  Pallas kernels  59.4 us (88%)
  local copies, waits for them, and re-layouts  6.5 us (10%)
    pallas_call x1, Pallas kernels, local(): pl.pallas_call(functools.partial(kernel, (n, nb, levels, block_len)), out...  59.4 us
    unnamed x6, local copies, waits for them, and re-layouts  6.5 us

commit v1 on v0

v1 whole, which is shorter than its diff:
```python
import functools
import math

import jax
import jax.numpy as jnp
from jax import lax
from jax.experimental import pallas as pl
from jax.experimental.pallas import tpu as pltpu
from jax.sharding import PartitionSpec as P

MESH = pl.DeviceIdType.MESH
FULL = 32760.0
LOW = -1e30
PIECES = 4
LATE = 3
STEP_UNIT = float(1 << 18)
D_TIME, D_GAP = 3.6, 4.5
RELAY_TIME, ATTEND_TIME, ATTEND_GAP = 11.5, 13.0, 1.4
FOLD_TIME, FOLD_GAP, LEVEL_GAP = 10.4, 1.4, 6.0
LATE_TIME, LATE_GAP, LAST_GAP = 15.0, 4.5, 2.0


def to_int16(value):
    return jnp.round(value).astype(jnp.int32).astype(jnp.int16)


def to_float(value):
    return value.astype(jnp.int32).astype(jnp.float32)


def tile_lanes(row, width):
    return jnp.concatenate([row] * (width // 128), axis=1)


def lane_top(values):
    top = jnp.abs(values[0])
    for value in values[1:]:
        top = jnp.maximum(top, jnp.abs(value))
    parts = [top[:, i : i + 128] for i in range(0, top.shape[1], 128)]
    top = parts[0]
    for part in parts[1:]:
        top = jnp.maximum(top, part)
    return jnp.maximum(jnp.max(top, axis=0, keepdims=True), 1e-30)


def split_rows(value, size, bit):
    count = value.shape[0] // size
    even = [value[k * size : (k + 1) * size] for k in range(0, count, 2)]
    odd = [value[k * size : (k + 1) * size] for k in range(1, count, 2)]
    even = jnp.concatenate(even, axis=0) if len(even) > 1 else even[0]
    odd = jnp.concatenate(odd, axis=0) if len(odd) > 1 else odd[0]
    right = jnp.full(even.shape, bit, jnp.int32) == 1
    return jnp.where(right, odd, even), jnp.where(right, even, odd)


def pick(r, b, requests, all_prompts, plen, tslot, clen):
    slot = b * requests + r
    chosen, length, hits = jnp.int32(0), jnp.int32(0), jnp.int32(0)
    for p in range(all_prompts):
        hit = tslot[p] == slot
        chosen = jnp.where(hit, p, chosen)
        length = jnp.where(hit, plen[p], length)
        hits = jnp.where(hit, 1, hits)
    return chosen, hits, jnp.where(hits > 0, length, clen[r])


def exchange(dims, *refs):
    n, nb, levels, block_len, late_units = dims
    refs = list(refs)

    def take(count):
        out = refs[:count]
        del refs[:count]
        return out

    scalar_hbm = take(3)
    cache_hbm, states_hbm, steps_hbm, resident_hbm, token_hbm, queries_hbm, rates_hbm = take(7)
    through_hbm = take(7)
    merged, handed, orecv, lse_recv, rates_own = take(5)
    through = take(7)
    arrived, cache_send, states, steps, resident, token, queries, rates, osend, lse_all, lse_send = take(11)
    plen, tslot, clen = scalars = take(3)
    load_sems, state_sems, piece_sems, through_sems = take(4)
    d_send, d_recv, d_sel = take(levels), take(levels), take(levels)
    d_keep = take(levels - 1)
    q_send, q_recv = take(levels), take(levels)
    acc = take(levels - 1)
    m_send, m_recv = take(2)
    if late_units:
        zm_send, zm_recv, zsteps_send, zsteps_recv, zpre, zbuf = take(6)
        zd_send, zd_recv, zd_sel, zd_keep = (take(levels - 1) for _ in range(4))
        zd_ss, zd_rs, zm_ss, zm_rs = take(4)
    (
        cache_ss, cache_rs, relay_ss, relay_rs, d_ss, d_rs, q_ss, q_rs, m_ss, m_rs,
        hand_ss, hand_rs, o_ss, o_rs, l_ss, l_rs,
    ) = refs

    me = lax.axis_index("seq")
    b = lax.axis_index("batch")
    prompts, rows, _, kv_heads, width = cache_hbm.shape
    all_prompts = prompts * nb
    requests, heads, head_dim = queries.shape
    state_n, channels = rates.shape
    share_len = channels // n
    piece = share_len // PIECES
    own_heads = heads // n
    group = heads // kv_heads
    positions = resident.shape[1]
    bits = [lax.rem(me // (1 << s), 2) for s in range(levels)]
    peers = [me + (1 - 2 * bits[s]) * (1 << s) for s in range(levels)]
    first = b * prompts

    barrier = pltpu.get_barrier_semaphore()
    for k in range(1, n):
        pl.semaphore_signal(barrier, inc=1, device_id={"seq": lax.rem(me + k, n)}, device_id_type=MESH)
    for k in range(1, nb):
        pl.semaphore_signal(barrier, inc=1, device_id={"batch": lax.rem(b + k, nb)}, device_id_type=MESH)

    def load(src, dst, sem):
        copy = pltpu.make_async_copy(src, dst, sem)
        copy.start()
        return copy

    load_scalars = [load(src, dst, load_sems.at[6 + i]) for i, (src, dst) in enumerate(zip(scalar_hbm, scalars))]
    load_steps = load(steps_hbm, steps, load_sems.at[0])
    load_pieces = []
    for k in list(range(1, n)) + [0]:
        to = lax.rem(me + k, n)
        dst = cache_send.at[to] if k else arrived.at[b, me]
        load_pieces.append(load(cache_hbm.at[:, :, to], dst, piece_sems.at[k]))
    load_states = [load(states_hbm.at[0], states.at[0], state_sems.at[0])]
    load_rates = load(rates_hbm, rates, load_sems.at[1])
    for p in range(1, prompts):
        load_states.append(load(states_hbm.at[p], states.at[p], state_sems.at[p]))
    load_attention = [
        load(resident_hbm, resident, load_sems.at[2]),
        load(token_hbm, token, load_sems.at[3]),
        load(queries_hbm, queries, load_sems.at[4]),
    ]
    own_lanes = pl.ds(pl.multiple_of(me * share_len, 128), share_len)
    load_through = [load(rates_hbm.at[:, own_lanes], rates_own, load_sems.at[5])]
    for i, (src, dst) in enumerate(zip(through_hbm, through)):
        load_through.append(load(src, dst, through_sems.at[i]))

    def remote(src, dst, ss, rs, where):
        return pltpu.make_async_remote_copy(
            src_ref=src, dst_ref=dst, send_sem=ss, recv_sem=rs, device_id=where, device_id_type=MESH
        )

    def start(copy):
        copy.start()
        return copy

    def settle(ref, sem):
        pltpu.make_async_copy(ref, ref, sem).wait()

    def lanes(share, h):
        return pl.ds(pl.multiple_of(share * share_len + h * piece, 128), piece)

    for copy in load_scalars:
        copy.wait()
    usable = [
        jnp.where(me * block_len < plen[first + p], 1.0, 0.0).astype(jnp.float32)
        for p in range(prompts)
    ]

    pl.semaphore_wait(barrier, n - 1 + nb - 1)

    def send_cache(k):
        to = lax.rem(me + k, n)
        load_pieces[k - 1].wait()
        start(remote(cache_send.at[to], arrived.at[b, me], cache_ss.at[0], cache_rs.at[0], {"seq": to}))

    for k in range(2, n, 2):
        send_cache(k)

    step_width = min(512, share_len)
    row_id = lax.broadcasted_iota(jnp.int32, (prompts, step_width), 0)
    usable_rows = jnp.zeros((prompts, step_width), jnp.float32)
    for p in range(prompts):
        usable_rows = jnp.where(row_id == p, usable[p], usable_rows)

    def step_rows(bit, c):
        parts = []
        for k in range(n // 2):
            at = pl.ds(pl.multiple_of((2 * k + bit) * share_len + c * step_width, 128), step_width)
            parts.append(jnp.concatenate([steps[p, :, at] for p in range(prompts)], axis=0) * usable_rows)
        return jnp.concatenate(parts, axis=0)

    def columns(c):
        return pl.ds(pl.multiple_of(c * step_width, 128), step_width)

    m_copies = [
        remote(m_send.at[s], m_recv.at[s], m_ss.at[s], m_rs.at[s], {"seq": peers[s]}) for s in range(levels)
    ]
    d_copies = [
        remote(d_send[s], d_recv[s], d_ss.at[s], d_rs.at[s], {"seq": peers[s]}) for s in range(levels)
    ]
    load_steps.wait()

    @pl.loop(0, share_len // step_width)
    def _(c):
        d_send[0][:, columns(c)] = to_int16(step_rows(1 - bits[0], c) * STEP_UNIT)

    start(d_copies[0])

    def fold_steps(s):
        d_copies[s].wait_recv()

        @pl.loop(0, share_len // step_width)
        def _(c):
            at = columns(c)
            other = to_float(d_recv[s][:, at]) * ((1 << s) / STEP_UNIT)
            own = step_rows(bits[0], c) if s == 0 else d_keep[s - 1][:, at]
            selected = jnp.where(jnp.full(own.shape, bits[s], jnp.int32) == 1, own, other)
            for k in range(n >> (s + 1)):
                d_sel[s][k, :, at] = selected[k * prompts : (k + 1) * prompts]
            if s + 1 < levels:
                keep, send = split_rows(own + other, prompts, bits[s + 1])
                d_keep[s][:, at] = keep
                d_send[s + 1][:, at] = to_int16(send * (STEP_UNIT / (1 << (s + 1))))

        m_copies[s].wait_recv()
        if s + 1 < levels:
            start(d_copies[s + 1])
            m_send[s + 1] = m_send[s] + m_recv[s]
            start(m_copies[s + 1])

    half = n // 2
    late_bits = bits[1:] + bits[:1]
    late_peers = peers[1:] + peers[:1]
    late_me = me // 2 + lax.rem(me, 2) * half
    units = [(p, h) for p in range(prompts) for h in range(PIECES)]
    total_units = len(units)
    plain = list(range(total_units - late_units))
    late = list(range(total_units - late_units, total_units))
    late_prompt = prompts - 1
    late_from = PIECES - late_units

    def is_late(u):
        return u >= total_units - late_units

    def bit_of(s, u):
        return late_bits[s] if is_late(u) else bits[s]

    def late_share(v):
        return lax.rem(v, half) * 2 + v // half

    q_copies = {}

    def send_values(s, u, values, factor):
        bound = zm_send[s] if is_late(u) else m_send[s, units[u][0] : units[u][0] + 1]
        scale = tile_lanes(FULL / bound * factor, piece)
        for k, value in enumerate(values):
            q_send[s][u, k] = to_int16(value * scale)
        where = {"seq": (late_peers if is_late(u) else peers)[s]}
        q_copies[s, u] = start(remote(q_send[s].at[u], q_recv[s].at[u], q_ss.at[s], q_rs.at[s, u], where))

    def read(s, u, k):
        p, h = units[u]
        if s > 0:
            return acc[s - 1][u, k]
        if is_late(u):
            return zbuf[h - late_from, 2 * k + late_bits[0]]
        return states[p, :, lanes(2 * k + bits[0], h)] * usable[p]

    def first_send(u):
        p, h = units[u]
        if is_late(u):
            values = [zbuf[h - late_from, 2 * k + 1 - late_bits[0]] for k in range(half)]
            send_values(0, u, values, 1.0)
        else:
            values = [states[p, :, lanes(2 * k + 1 - bits[0], h)] for k in range(half)]
            send_values(0, u, values, usable[p])

    def fold(s, u):
        p, h = units[u]
        q_copies[s, u].wait_recv()
        bound = zm_recv[s] if is_late(u) else m_recv[s, p : p + 1]
        scale = tile_lanes(bound * (1.0 / FULL), piece)
        right = jnp.full((state_n, piece), bit_of(s, u), jnp.int32) == 1
        below = lax.rem(late_me if is_late(u) else me, 1 << (s + 1))

        def folded(k):
            other = to_float(q_recv[s][u, k]) * scale
            own = read(s, u, k)
            if is_late(u) and s == levels - 1:
                return own + other
            v = k * (1 << (s + 1)) + below
            if is_late(u):
                share = late_share(v)
                late_at = (h - late_from) * piece
                behind = zd_sel[s][k][:, late_at : late_at + piece]
            else:
                share = v
                behind = d_sel[s][k, p : p + 1, h * piece : (h + 1) * piece]
            decay = jnp.exp(-rates[:, lanes(share, h)] * behind)
            early = jnp.where(right, other, own)
            later = jnp.where(right, own, other)
            return decay * early + later

        if s + 1 < levels:
            bit = bit_of(s + 1, u)
            count = n >> (s + 2)
            send_values(s + 1, u, [folded(2 * k + 1 - bit) for k in range(count)], 1.0)
            for k in range(count):
                acc[s][u, k] = folded(2 * k + bit)
        else:
            at = pl.ds(h * piece, piece)
            handed[first + p, :, at] = folded(0)
            for k in range(1, nb):
                start(
                    remote(
                        handed.at[first + p, :, at],
                        handed.at[first + p, :, at],
                        hand_ss.at[k - 1],
                        hand_rs.at[k - 1],
                        {"batch": lax.rem(b + k, nb)},
                    )
                )

    if late_units:
        late_lanes = late_units * piece

        def late_row(v):
            at = ((v % half) * 2 + v // half) * share_len + late_from * piece
            return steps[late_prompt, :, at : at + late_lanes]

        def late_rows():
            return jnp.concatenate([late_row(v) for v in range(n)], axis=0) * usable[late_prompt]

        zd_copies = [remote(zsteps_send, zsteps_recv, zd_ss.at[0], zd_rs.at[0], {"seq": peers[0]})]
        for i in range(levels - 1):
            zd_copies.append(
                remote(zd_send[i], zd_recv[i], zd_ss.at[i + 1], zd_rs.at[i + 1], {"seq": late_peers[i]})
            )
        zm_copies = [
            remote(zm_send.at[s], zm_recv.at[s], zm_ss.at[s], zm_rs.at[s], {"seq": late_peers[s]})
            for s in range(levels)
        ]
        zsteps_send[...] = to_int16(late_rows() * STEP_UNIT)
        start(zd_copies[0])

        def late_split(i, value):
            keep, send = split_rows(value, 1, late_bits[i])
            zd_keep[i][...] = keep
            zd_send[i][...] = send
            start(zd_copies[i + 1])

        def late_begin():
            zd_copies[0].wait_recv()
            other = to_float(zsteps_recv[...]) * (1.0 / STEP_UNIT)
            before = jnp.where(jnp.full(other.shape, bits[0], jnp.int32) == 1, 0.0, other)
            for v in range(n):
                zpre[v] = before[v : v + 1]
            late_split(0, late_rows() + other)

            @pl.loop(0, n)
            def _(v):
                row = zpre[v]
                for i in range(late_units):
                    at = lanes(late_share(v), late_from + i)
                    decay = jnp.exp(-rates[:, at] * row[:, i * piece : (i + 1) * piece])
                    zbuf[i, v] = states[late_prompt, :, at] * decay * usable[late_prompt]

            zm_send[0] = m_send[0, late_prompt : late_prompt + 1]
            start(zm_copies[0])
            for u in late:
                first_send(u)

        def late_steps(i):
            zd_copies[i + 1].wait_recv()
            zm_copies[i].wait_recv()
            zm_send[i + 1] = zm_send[i] + zm_recv[i]
            start(zm_copies[i + 1])
            own, other = zd_keep[i][...], zd_recv[i][...]
            selected = jnp.where(jnp.full(own.shape, late_bits[i], jnp.int32) == 1, own, other)
            for k in range(n >> (i + 1)):
                zd_sel[i][k] = selected[k : k + 1]
            if i + 1 < levels - 1:
                late_split(i + 1, own + other)

    for k in range(1, n, 2):
        send_cache(k)
    load_pieces[n - 1].wait()

    relays = [
        remote(
            arrived.at[b], arrived.at[b], relay_ss.at[k - 1], relay_rs.at[k - 1], {"batch": lax.rem(b + k, nb)}
        )
        for k in range(1, nb)
    ]

    top_width = min(512, share_len)
    for p in range(prompts):
        load_states[p].wait()

        def larger(i, top):
            at = pl.ds(pl.multiple_of(i * top_width, 128), top_width)
            return jnp.maximum(top, jnp.abs(states[p, :, at]))

        top = lax.fori_loop(0, channels // top_width, larger, jnp.zeros((state_n, top_width), jnp.float32), unroll=4)
        m_send[0, p : p + 1] = jnp.maximum(lane_top([top]) * usable[p], 1e-30)
    start(m_copies[0])
    for u in plain:
        first_send(u)

    shape3 = (positions, kv_heads, width)
    position = lax.broadcasted_iota(jnp.int32, shape3, 0) * n + me
    flat = positions * kv_heads
    column = lax.broadcasted_iota(jnp.int32, (heads, flat), 1)
    owner = lax.broadcasted_iota(jnp.int32, (heads, flat), 0) // group
    same_head = lax.rem(column, kv_heads) == owner
    column_position = (column // kv_heads) * n + me
    lane_id = lax.broadcasted_iota(jnp.int32, (heads, 128), 1)

    def attend(r):
        chosen, hits, length = pick(r, b, requests, all_prompts, plen, tslot, clen)
        fresh_limit = jnp.where(hits > 0, length, 0)
        new = arrived[chosen // prompts, :, lax.rem(chosen, prompts)].reshape(shape3).astype(jnp.float32)
        old = resident[r].astype(jnp.float32)
        x = jnp.where(position < fresh_limit, new, old)
        x = jnp.where(position < length, x, 0.0)
        x = jnp.where(position == length, token[r].astype(jnp.float32)[None], x)
        merged[r] = x.astype(jnp.bfloat16)
        x2 = x.reshape(flat, width)
        keys = x2[:, :head_dim].astype(jnp.bfloat16)
        values = x2[:, head_dim:].astype(jnp.bfloat16)
        score = lax.dot_general(
            queries[r], keys, (((1,), (1,)), ((), ())), preferred_element_type=jnp.float32
        ) * (1.0 / math.sqrt(head_dim))
        seen = same_head & (column_position <= length)
        score = jnp.where(seen, score, LOW)
        top = jnp.max(score, axis=1, keepdims=True)
        weight = jnp.where(seen, jnp.exp(score - top), 0.0)
        total = jnp.sum(weight, axis=1, keepdims=True)
        out = jnp.dot(weight.astype(jnp.bfloat16), values, preferred_element_type=jnp.float32)
        some = total > 0.0
        safe = jnp.where(some, total, 1.0)
        out = out / safe
        lse = jnp.where(some, top + jnp.log(safe), LOW)
        peak = jnp.maximum(jnp.max(jnp.abs(out), axis=1, keepdims=True), 1e-30)
        coded = jnp.round(out * (FULL / peak)).astype(jnp.int32)
        for j in range(n):
            osend[j, r * own_heads : (r + 1) * own_heads] = coded[j * own_heads : (j + 1) * own_heads].astype(jnp.int16)
        noted = jnp.where(lane_id == r, lse, lse_all[...])
        lse_all[...] = jnp.where(lane_id == requests + r, peak * (1.0 / FULL), noted)

    def attention_begin():
        settle(arrived.at[b, pl.ds(0, n - 1)], cache_rs.at[0])
        for copy in relays:
            start(copy)
        for copy in load_attention:
            copy.wait()
        lse_all[...] = jnp.zeros((heads, 128), jnp.float32)

    def attention_end():
        for j in range(n):
            lse_send[j] = lse_all[j * own_heads : (j + 1) * own_heads]
        for k in range(1, n):
            to = lax.rem(me + k, n)
            start(remote(lse_send.at[to], lse_recv.at[me], l_ss.at[0], l_rs.at[0], {"seq": to}))
            start(remote(osend.at[to], orecv.at[me], o_ss.at[0], o_rs.at[0], {"seq": to}))
        lse_recv[me] = lse_send[me]
        orecv[me] = osend[me]

    load_rates.wait()

    def attend_some(r):
        if r == 0:
            for copy in relays:
                copy.wait_recv()
        attend(r)
        if r == requests - 1:
            attention_end()

    def fold_late(s):
        if s == levels - 1:
            zm_copies[s].wait_recv()
        for u in late:
            fold(s, u)

    events = [(D_TIME + D_GAP * s, functools.partial(fold_steps, s)) for s in range(levels)]
    events.append((RELAY_TIME, attention_begin))
    events += [(ATTEND_TIME + ATTEND_GAP * r, functools.partial(attend_some, r)) for r in range(requests)]
    for i, u in enumerate(plain):
        for s in range(levels):
            events.append((FOLD_TIME + FOLD_GAP * i + LEVEL_GAP * s, functools.partial(fold, s, u)))
    if late_units:
        events.append((D_TIME + 0.1, late_begin))
        for s in range(1, levels):
            events.append((D_TIME + D_GAP * s + 0.1, functools.partial(late_steps, s - 1)))
            events.append((LATE_TIME + LATE_GAP * (s - 1), functools.partial(fold_late, s - 1)))
        last = FOLD_TIME + FOLD_GAP * len(plain) + LAST_GAP
        events.append((last, functools.partial(fold_late, levels - 1)))
    for _, event in sorted(events, key=lambda e: e[0]):
        event()

    for copy in load_through:
        copy.wait()
    others = pl.ds(0, n - 1)
    settle(lse_recv.at[others], l_rs.at[0])
    settle(orecv.at[others], o_rs.at[0])
    for k in range(1, nb):
        theirs = pl.ds(lax.rem(b + nb - k, nb) * prompts, prompts)
        settle(handed.at[theirs], hand_rs.at[k - 1])
        settle(handed.at[pl.ds(first, prompts)], hand_ss.at[k - 1])
    settle(cache_send.at[others], cache_ss.at[0])
    settle(lse_send.at[others], l_ss.at[0])
    settle(osend.at[others], o_ss.at[0])
    for s in range(levels):
        settle(q_send[s], q_ss.at[s])
    for copy in relays + d_copies + m_copies + (zd_copies + zm_copies if late_units else []):
        copy.wait_send()


def finish(dims, plen, tslot, clen, merged, handed, orecv, lse_recv, rates, rstates, dt, inner, gate, s_in, s_out, skip,
           merged_out, attention_out, nstates_out, mout_out, nstates, mout, attention, sems):
    n, nb = dims
    b = lax.axis_index("batch")
    all_prompts = handed.shape[0]
    requests, state_n, share_len = rstates.shape
    own_heads, head_dim = attention.shape[1:]
    chunk = min(512, share_len)
    per_share = share_len // chunk

    copies = []

    def out(src, dst, i):
        copy = pltpu.make_async_copy(src, dst, sems.at[i])
        copy.start()
        copies.append(copy)

    out(merged, merged_out, 0)
    eye = lax.broadcasted_iota(jnp.int32, (state_n, state_n), 0) == lax.broadcasted_iota(
        jnp.int32, (state_n, state_n), 1
    )

    def as_column(row):
        spread = jnp.where(eye, jnp.broadcast_to(row, (state_n, state_n)), 0.0)
        return jnp.sum(spread, axis=1, keepdims=True)

    picks = [pick(r, b, requests, all_prompts, plen, tslot, clen) for r in range(requests)]
    in_all, out_all = s_in[...], s_out[...]
    in_cols = [as_column(in_all[r : r + 1]) for r in range(requests)]
    out_cols = [as_column(out_all[r : r + 1]) for r in range(requests)]

    for c in range(per_share):
        at = pl.ds(c * chunk, chunk)
        step_rows = dt[:, at]
        x_rows = inner[:, at].astype(jnp.float32)
        g = gate[:, at].astype(jnp.float32)
        rate = -rates[:, at]
        push_rows = step_rows * x_rows
        out_rows = []
        for r in range(requests):
            chosen, hits, _ = picks[r]
            fresh = jnp.full((state_n, chunk), hits, jnp.int32) > 0
            begin = jnp.where(fresh, handed[chosen, :, at], rstates[r, :, at])
            after = jnp.exp(rate * step_rows[r : r + 1]) * begin
            after = after + push_rows[r : r + 1] * in_cols[r]
            nstates[r, :, at] = after
            out_rows.append(jnp.sum(out_cols[r] * after, axis=0, keepdims=True))
        out(nstates.at[:, :, at], nstates_out.at[:, :, at], 3 + c)
        read_out = jnp.concatenate(out_rows, axis=0) + skip[:, at] * x_rows
        mout[:, at] = (read_out * (g / (1.0 + jnp.exp(-g)))).astype(jnp.bfloat16)
    out(mout, mout_out, 1)

    lane3 = lax.broadcasted_iota(jnp.int32, (n, own_heads, 128), 2)
    noted = lse_recv[...]
    for r in range(requests):
        lse = jnp.sum(jnp.where(lane3 == r, noted, 0.0), axis=2, keepdims=True)
        unit = jnp.sum(jnp.where(lane3 == requests + r, noted, 0.0), axis=2, keepdims=True)
        share = jnp.exp(lse - jnp.max(lse, axis=0, keepdims=True))
        parts = to_float(orecv[:, r * own_heads : (r + 1) * own_heads])
        top = jnp.sum(share * unit * parts, axis=0)
        attention[r] = (top / jnp.sum(share, axis=0)).astype(jnp.bfloat16)
    out(attention, attention_out, 2)
    for copy in copies:
        copy.wait()


def local(
    n,
    nb,
    prompt_cache,
    prompt_states,
    block_steps,
    prompt_lengths,
    target_slots,
    cache_lengths,
    resident_cache,
    token_cache,
    queries,
    resident_states,
    decay_rates,
    step_sizes,
    inner_input,
    inner_gate,
    state_input,
    state_readout,
    skip_gain,
):
    levels = n.bit_length() - 1
    prompts, block_len, kv_heads, width = prompt_cache.shape
    requests, heads, head_dim = queries.shape
    state_n, channels = decay_rates.shape
    share = channels // n
    piece = share // PIECES
    own_heads = heads // n
    positions = resident_cache.shape[1]
    all_prompts = prompts * nb
    rows = block_len // n
    unit_count = prompts * PIECES
    late_units = LATE
    f32, bf16, i16 = jnp.float32, jnp.bfloat16, jnp.int16
    vmem = pl.BlockSpec(memory_space=pltpu.VMEM)
    smem = pl.BlockSpec(memory_space=pltpu.SMEM)
    hbm = pl.BlockSpec(memory_space=pltpu.HBM)
    dma = pltpu.SemaphoreType.DMA
    halves = [n >> (s + 1) for s in range(levels)]
    through = (resident_states, step_sizes, inner_input, inner_gate, state_input, state_readout, skip_gain[None])
    operands = (
        prompt_cache.reshape(prompts, rows, n, kv_heads, width),
        prompt_states[:, 0],
        block_steps,
        resident_cache[:, :, 0],
        token_cache,
        queries,
        decay_rates,
    ) + through
    outs = (
        pltpu.VMEM((requests, positions, kv_heads, width), bf16),
        pltpu.VMEM((all_prompts, state_n, share), f32),
        pltpu.VMEM((n, requests * own_heads, head_dim), i16),
        pltpu.VMEM((n, own_heads, 128), f32),
        pltpu.VMEM((state_n, share), f32),
    ) + tuple(pltpu.VMEM(x.shape, x.dtype) for x in through)
    scratch = [
        pltpu.VMEM((nb, n, prompts, rows, kv_heads, width), bf16),
        pltpu.VMEM((n, prompts, rows, kv_heads, width), bf16),
        pltpu.VMEM((prompts, state_n, channels), f32),
        pltpu.VMEM(block_steps.shape, f32),
        pltpu.VMEM((requests, positions, kv_heads, width), bf16),
        pltpu.VMEM(token_cache.shape, bf16),
        pltpu.VMEM(queries.shape, bf16),
        pltpu.VMEM(decay_rates.shape, f32),
        pltpu.VMEM((n, requests * own_heads, head_dim), i16),
        pltpu.VMEM((heads, 128), f32),
        pltpu.VMEM((n, own_heads, 128), f32),
        pltpu.SMEM(prompt_lengths.shape, jnp.int32),
        pltpu.SMEM(target_slots.shape, jnp.int32),
        pltpu.SMEM(cache_lengths.shape, jnp.int32),
        dma((9,)),
        dma((prompts,)),
        dma((n,)),
        dma((len(through),)),
    ]
    for _ in range(2):
        scratch += [pltpu.VMEM((h * prompts, share), i16) for h in halves]
    scratch += [pltpu.VMEM((h, prompts, share), f32) for h in halves]
    scratch += [pltpu.VMEM((h * prompts, share), f32) for h in halves[1:]]
    for _ in range(2):
        scratch += [pltpu.VMEM((unit_count, h, state_n, piece), i16) for h in halves]
    scratch += [pltpu.VMEM((unit_count, h, state_n, piece), f32) for h in halves[1:]]
    scratch += [pltpu.VMEM((levels, prompts, 128), f32)] * 2
    if late_units:
        late_lanes = late_units * piece
        scratch += [pltpu.VMEM((levels, 1, 128), f32)] * 2
        scratch += [pltpu.VMEM((n, late_lanes), i16)] * 2
        scratch += [pltpu.VMEM((n, 1, late_lanes), f32)]
        scratch += [pltpu.VMEM((late_units, n, state_n, piece), f32)]
        for _ in range(2):
            scratch += [pltpu.VMEM((h, late_lanes), f32) for h in halves[: levels - 1]]
        scratch += [pltpu.VMEM((h, 1, late_lanes), f32) for h in halves[: levels - 1]]
        scratch += [pltpu.VMEM((h, late_lanes), f32) for h in halves[: levels - 1]]
        scratch += [dma((levels,))] * 4
    scratch += [dma((1,))] * 2
    scratch += [dma((max(nb - 1, 1),))] * 2
    scratch += [dma((levels,))] * 2
    scratch += [dma((levels,)), dma((levels, unit_count))]
    scratch += [dma((levels,))] * 2
    scratch += [dma((max(nb - 1, 1),))] * 2
    scratch += [dma((1,))] * 4
    scalars = [
        pltpu.with_memory_space_constraint(x, pltpu.HBM)
        for x in (prompt_lengths, target_slots, cache_lengths)
    ]
    parts = pl.pallas_call(
        functools.partial(exchange, (n, nb, levels, block_len, late_units)),
        out_shape=outs,
        in_specs=[hbm] * (3 + len(operands)),
        out_specs=(vmem,) * len(outs),
        scratch_shapes=scratch,
        compiler_params=pltpu.CompilerParams(
            collective_id=0, has_side_effects=True, vmem_limit_bytes=40 << 20
        ),
    )(*scalars, *(pltpu.with_memory_space_constraint(x, pltpu.HBM) for x in operands))
    chunks = share // min(512, share)
    merged, attention, next_states, mamba_output = pl.pallas_call(
        functools.partial(finish, (n, nb)),
        out_shape=(
            jax.ShapeDtypeStruct((requests, positions, kv_heads, width), bf16),
            jax.ShapeDtypeStruct((requests, own_heads, head_dim), bf16),
            jax.ShapeDtypeStruct((requests, state_n, share), f32),
            jax.ShapeDtypeStruct((requests, share), bf16),
        ),
        in_specs=[smem] * 3 + [vmem] * len(parts),
        out_specs=(hbm,) * 4,
        scratch_shapes=[
            pltpu.VMEM((requests, state_n, share), f32),
            pltpu.VMEM((requests, share), bf16),
            pltpu.VMEM((requests, own_heads, head_dim), bf16),
            dma((3 + chunks,)),
        ],
        compiler_params=pltpu.CompilerParams(vmem_limit_bytes=16 << 20),
    )(*scalars, *parts)
    return merged[:, :, None], attention, next_states, mamba_output


def solution(mesh):
    n, nb = mesh.shape["seq"], mesh.shape["batch"]
    return jax.shard_map(
        functools.partial(local, n, nb),
        mesh=mesh,
        in_specs=(
            P(("groups", "batch"), "seq", None, None),
            P(("groups", "batch"), "seq", None, None),
            P(("groups", "batch"), "seq", None),
            P("groups"),
            P("groups"),
            P(("groups", "batch")),
            P(("groups", "batch"), None, "seq", None, None),
            P(("groups", "batch"), None, None),
            P(("groups", "batch"), None, None),
            P(("groups", "batch"), None, "seq"),
            P(),
            P(("groups", "batch"), "seq"),
            P(("groups", "batch"), "seq"),
            P(("groups", "batch"), "seq"),
            P(("groups", "batch"), None),
            P(("groups", "batch"), None),
            P("seq"),
        ),
        out_specs=(
            P(("groups", "batch"), None, "seq", None, None),
            P(("groups", "batch"), "seq", None),
            P(("groups", "batch"), None, "seq"),
            P(("groups", "batch"), "seq"),
        ),
        check_vma=False,
    )
```

time: 67.5 us -> 47.7 us (0.71); the launches traced: 66.5 us -> 47.6 us
  Pallas kernels: 59.4 us -> 46.9 us
  local copies, waits for them, and re-layouts: 6.5 us -> 0 us
    pallas_call x1 -> x2, Pallas kernels: 59.4 us -> 46.9 us  [the longest x1 44.7 us: local(): pl.pallas_call(functools.partial(exchange, (n, nb, levels, block_len, lat...]
    unnamed x6 -> x0, local copies, waits for them, and re-layouts: 6.5 us -> none
where the time goes in v1:
time: 47.7 us; the launch traced here: 47.6 us
  Pallas kernels  46.9 us (98%)
  between operations  0.64 us (1%)
    pallas_call x1, Pallas kernels, local(): pl.pallas_call(functools.partial(exchange, (n, nb, levels, block_len, lat...  44.7 us
    pallas_call x1, Pallas kernels, local(): pl.pallas_call(functools.partial(finish, (n, nb)), out_shape=(jax.ShapeDt...  2.19 us

profile of v1, /device:TPU:0, one launch (start us, length us, event | category | flops | bytes accessed | tf_op | source)
XLA Modules:
  0.0 47.6 jit_solution(7274235982786130866)
XLA Ops:
  0.6 44.7 %shard_map.192 = (bf16[8,32,8,256]{3,2,1,0:T(8,128)(2,1)S(1)}, f32[8,16,2048]{2,1,0:T(8,128)S(1)}, s16[8,64,128]{2,1,0:T(8,128)(2,1)S(1)}, f32[8,8,128]{2,1,0:T(...) custom-call(s32[8]{0:T(128)} %plen.1, s32[8]{0:T(128)} %tslot.1, ...), custom_call_target="tpu_custom_call" | custom-call | tf_op jit(solution)/shard_map/pallas_call | solution.py:689
  45.4 2.2 %shard_map.193 = (bf16[8,32,8,256]{3,2,1,0:T(8,128)(2,1)}, bf16[8,8,128]{2,1,0:T(8,128)(2,1)}, f32[8,16,2048]{2,1,0:T(8,128)}, bf16[8,2048]{1,0:T(8,128)(2,1)}) custom-call(s32[8]{0:T(128)} %plen.1, s32[8]{0:T(128)} %tslot.1, s32[8]{0:T(128)} %clen.1, bf16[8,32,8,256]{3,2,1,0:T(8,128)(2,1)S(1)} %get-tuple-element.20.merged, ...), custom_call_target="tpu_custom_call" | custom-call | tf_op jit(solution)/shard_map/pallas_call | solution.py:700

commit v2 on v1

--- a/solution.py
+++ b/solution.py
@@ -12,12 +12,14 @@
 FULL = 32760.0
 LOW = -1e30
 PIECES = 4
-LATE = 3
+LATE = 2
 STEP_UNIT = float(1 << 18)
-D_TIME, D_GAP = 3.6, 4.5
-RELAY_TIME, ATTEND_TIME, ATTEND_GAP = 11.5, 13.0, 1.4
-FOLD_TIME, FOLD_GAP, LEVEL_GAP = 10.4, 1.4, 6.0
-LATE_TIME, LATE_GAP, LAST_GAP = 15.0, 4.5, 2.0
+D_TIME, D_GAP = 4.5, 4.6
+BOUND_TIME, BOUND_GAP = 6.5, 3.5
+RELAY_TIME, ATTEND_TIME, ATTEND_GAP = 14.5, 15.5, 0.5
+OUT_TIME, OUT_GAP = 19.5, 0.05
+FOLD_TIME, FOLD_GAP, FIRST_LAG, NEXT_LAG = 8.8, 1.39, 5.5, 5.5
+LATE_TIME, LATE_GAP, LAST_GAP = 16.0, 0.5, 4.0
 
 
 def to_int16(value):
@@ -78,18 +80,18 @@
     through_hbm = take(7)
     merged, handed, orecv, lse_recv, rates_own = take(5)
     through = take(7)
-    arrived, cache_send, states, steps, resident, token, queries, rates, osend, lse_all, lse_send = take(11)
+    arrived, states, steps, resident, token, queries, rates, osend, lse_all, lse_send = take(10)
     plen, tslot, clen = scalars = take(3)
-    load_sems, state_sems, piece_sems, through_sems = take(4)
+    load_sems, state_sems, through_sems = take(3)
     d_send, d_recv, d_sel = take(levels), take(levels), take(levels)
     d_keep = take(levels - 1)
     q_send, q_recv = take(levels), take(levels)
     acc = take(levels - 1)
-    m_send, m_recv = take(2)
+    table, bound_own, bound_peer = take(3)
     if late_units:
-        zm_send, zm_recv, zsteps_send, zsteps_recv, zpre, zbuf = take(6)
-        zd_send, zd_recv, zd_sel, zd_keep = (take(levels - 1) for _ in range(4))
-        zd_ss, zd_rs, zm_ss, zm_rs = take(4)
+        late_own, late_peer, zsteps_send, zsteps_recv, zpre = take(5)
+        zd_send, zd_recv, zd_sel, zd_keep = take(4)
+        zd_ss, zd_rs = take(2)
     (
         cache_ss, cache_rs, relay_ss, relay_rs, d_ss, d_rs, q_ss, q_rs, m_ss, m_rs,
         hand_ss, hand_rs, o_ss, o_rs, l_ss, l_rs,
@@ -123,12 +125,8 @@
 
     load_scalars = [load(src, dst, load_sems.at[6 + i]) for i, (src, dst) in enumerate(zip(scalar_hbm, scalars))]
     load_steps = load(steps_hbm, steps, load_sems.at[0])
-    load_pieces = []
-    for k in list(range(1, n)) + [0]:
-        to = lax.rem(me + k, n)
-        dst = cache_send.at[to] if k else arrived.at[b, me]
-        load_pieces.append(load(cache_hbm.at[:, :, to], dst, piece_sems.at[k]))
     load_states = [load(states_hbm.at[0], states.at[0], state_sems.at[0])]
+    load_piece = load(cache_hbm.at[:, :, me], arrived.at[b, me], load_sems.at[9])
     load_rates = load(rates_hbm, rates, load_sems.at[1])
     for p in range(1, prompts):
         load_states.append(load(states_hbm.at[p], states.at[p], state_sems.at[p]))
@@ -157,6 +155,24 @@
     def lanes(share, h):
         return pl.ds(pl.multiple_of(share * share_len + h * piece, 128), piece)
 
+    pl.semaphore_wait(barrier, n - 1 + nb - 1)
+
+    def across(k):
+        to = me
+        for i in range(levels):
+            if (k >> i) % 2:
+                to = to + peers[i] - me
+        return to
+
+    def send_cache(k):
+        to = across(k)
+        start(remote(cache_hbm.at[:, :, to], arrived.at[b, me], cache_ss.at[0], cache_rs.at[0], {"seq": to}))
+
+    for k in range(n - 1, 1, -2):
+        send_cache(k)
+    for k in range(n - 2, 0, -2):
+        send_cache(k)
+
     for copy in load_scalars:
         copy.wait()
     usable = [
@@ -164,16 +180,6 @@
         for p in range(prompts)
     ]
 
-    pl.semaphore_wait(barrier, n - 1 + nb - 1)
-
-    def send_cache(k):
-        to = lax.rem(me + k, n)
-        load_pieces[k - 1].wait()
-        start(remote(cache_send.at[to], arrived.at[b, me], cache_ss.at[0], cache_rs.at[0], {"seq": to}))
-
-    for k in range(2, n, 2):
-        send_cache(k)
-
     step_width = min(512, share_len)
     row_id = lax.broadcasted_iota(jnp.int32, (prompts, step_width), 0)
     usable_rows = jnp.zeros((prompts, step_width), jnp.float32)
@@ -190,9 +196,6 @@
     def columns(c):
         return pl.ds(pl.multiple_of(c * step_width, 128), step_width)
 
-    m_copies = [
-        remote(m_send.at[s], m_recv.at[s], m_ss.at[s], m_rs.at[s], {"seq": peers[s]}) for s in range(levels)
-    ]
     d_copies = [
         remote(d_send[s], d_recv[s], d_ss.at[s], d_rs.at[s], {"seq": peers[s]}) for s in range(levels)
     ]
@@ -220,16 +223,33 @@
                 d_keep[s][:, at] = keep
                 d_send[s + 1][:, at] = to_int16(send * (STEP_UNIT / (1 << (s + 1))))
 
-        m_copies[s].wait_recv()
         if s + 1 < levels:
             start(d_copies[s + 1])
-            m_send[s + 1] = m_send[s] + m_recv[s]
-            start(m_copies[s + 1])
+
+    def bottom(device, s):
+        return device - lax.rem(device, 1 << s)
+
+    def fold_bounds(s):
+        settle(table.at[pl.ds(0, 1 << s)], m_rs.at[s])
+
+        def group_bound(device):
+            total = table[bottom(device, s)]
+            for i in range(1, 1 << s):
+                total = total + table[bottom(device, s) + i]
+            return total
+
+        bound_peer[s] = group_bound(peers[s])
+        if s + 1 < levels:
+            bound_own[s + 1] = bound_own[s] + bound_peer[s]
+        if late_units and s == 1:
+            at = slice(late_prompt, late_prompt + 1)
+            late_own[1] = table[me, at] + table[peers[1], at]
+            late_peer[0] = table[peers[1], at]
+            late_peer[1] = table[peers[0], at] + table[peers[0] + peers[1] - me, at]
 
     half = n // 2
-    late_bits = bits[1:] + bits[:1]
-    late_peers = peers[1:] + peers[:1]
-    late_me = me // 2 + lax.rem(me, 2) * half
+    late_bits = [bits[1], bits[0]] + bits[2:]
+    late_peers = [peers[1], peers[0]] + peers[2:]
     units = [(p, h) for p in range(prompts) for h in range(PIECES)]
     total_units = len(units)
     plain = list(range(total_units - late_units))
@@ -244,12 +264,12 @@
         return late_bits[s] if is_late(u) else bits[s]
 
     def late_share(v):
-        return lax.rem(v, half) * 2 + v // half
+        return (v // 4) * 4 + (v % 2) * 2 + (v // 2) % 2
 
     q_copies = {}
 
     def send_values(s, u, values, factor):
-        bound = zm_send[s] if is_late(u) else m_send[s, units[u][0] : units[u][0] + 1]
+        bound = late_own[s] if is_late(u) and s < 2 else bound_own[s, units[u][0] : units[u][0] + 1]
         scale = tile_lanes(FULL / bound * factor, piece)
         for k, value in enumerate(values):
             q_send[s][u, k] = to_int16(value * scale)
@@ -261,14 +281,13 @@
         if s > 0:
             return acc[s - 1][u, k]
         if is_late(u):
-            return zbuf[h - late_from, 2 * k + late_bits[0]]
+            return late_value(u, 2 * k + late_bits[0])
         return states[p, :, lanes(2 * k + bits[0], h)] * usable[p]
 
     def first_send(u):
         p, h = units[u]
         if is_late(u):
-            values = [zbuf[h - late_from, 2 * k + 1 - late_bits[0]] for k in range(half)]
-            send_values(0, u, values, 1.0)
+            send_values(0, u, [late_value(u, 2 * k + 1 - late_bits[0]) for k in range(half)], 1.0)
         else:
             values = [states[p, :, lanes(2 * k + 1 - bits[0], h)] for k in range(half)]
             send_values(0, u, values, usable[p])
@@ -276,23 +295,22 @@
     def fold(s, u):
         p, h = units[u]
         q_copies[s, u].wait_recv()
-        bound = zm_recv[s] if is_late(u) else m_recv[s, p : p + 1]
+        bound = late_peer[s] if is_late(u) and s < 2 else bound_peer[s, p : p + 1]
         scale = tile_lanes(bound * (1.0 / FULL), piece)
         right = jnp.full((state_n, piece), bit_of(s, u), jnp.int32) == 1
-        below = lax.rem(late_me if is_late(u) else me, 1 << (s + 1))
+        below = lax.rem(late_share(me) if is_late(u) else me, 1 << (s + 1))
 
         def folded(k):
             other = to_float(q_recv[s][u, k]) * scale
             own = read(s, u, k)
-            if is_late(u) and s == levels - 1:
+            if is_late(u) and s == 1:
                 return own + other
             v = k * (1 << (s + 1)) + below
-            if is_late(u):
-                share = late_share(v)
+            share = late_share(v) if is_late(u) else v
+            if is_late(u) and s == 0:
                 late_at = (h - late_from) * piece
-                behind = zd_sel[s][k][:, late_at : late_at + piece]
+                behind = zd_sel[k][:, late_at : late_at + piece]
             else:
-                share = v
                 behind = d_sel[s][k, p : p + 1, h * piece : (h + 1) * piece]
             decay = jnp.exp(-rates[:, lanes(share, h)] * behind)
             early = jnp.where(right, other, own)
@@ -323,29 +341,25 @@
         late_lanes = late_units * piece
 
         def late_row(v):
-            at = ((v % half) * 2 + v // half) * share_len + late_from * piece
+            at = late_share(v) * share_len + late_from * piece
             return steps[late_prompt, :, at : at + late_lanes]
 
         def late_rows():
             return jnp.concatenate([late_row(v) for v in range(n)], axis=0) * usable[late_prompt]
 
-        zd_copies = [remote(zsteps_send, zsteps_recv, zd_ss.at[0], zd_rs.at[0], {"seq": peers[0]})]
-        for i in range(levels - 1):
-            zd_copies.append(
-                remote(zd_send[i], zd_recv[i], zd_ss.at[i + 1], zd_rs.at[i + 1], {"seq": late_peers[i]})
-            )
-        zm_copies = [
-            remote(zm_send.at[s], zm_recv.at[s], zm_ss.at[s], zm_rs.at[s], {"seq": late_peers[s]})
-            for s in range(levels)
+        zd_copies = [
+            remote(zsteps_send, zsteps_recv, zd_ss.at[0], zd_rs.at[0], {"seq": peers[0]}),
+            remote(zd_send, zd_recv, zd_ss.at[1], zd_rs.at[1], {"seq": late_peers[0]}),
         ]
         zsteps_send[...] = to_int16(late_rows() * STEP_UNIT)
         start(zd_copies[0])
 
-        def late_split(i, value):
-            keep, send = split_rows(value, 1, late_bits[i])
-            zd_keep[i][...] = keep
-            zd_send[i][...] = send
-            start(zd_copies[i + 1])
+        def late_value(u, v):
+            h = units[u][1]
+            at = lanes(late_share(v), h)
+            late_at = (h - late_from) * piece
+            decay = jnp.exp(-rates[:, at] * zpre[v][:, late_at : late_at + piece])
+            return states[late_prompt, :, at] * (decay * usable[late_prompt])
 
         def late_begin():
             zd_copies[0].wait_recv()
@@ -353,36 +367,22 @@
             before = jnp.where(jnp.full(other.shape, bits[0], jnp.int32) == 1, 0.0, other)
             for v in range(n):
                 zpre[v] = before[v : v + 1]
-            late_split(0, late_rows() + other)
-
-            @pl.loop(0, n)
-            def _(v):
-                row = zpre[v]
-                for i in range(late_units):
-                    at = lanes(late_share(v), late_from + i)
-                    decay = jnp.exp(-rates[:, at] * row[:, i * piece : (i + 1) * piece])
-                    zbuf[i, v] = states[late_prompt, :, at] * decay * usable[late_prompt]
-
-            zm_send[0] = m_send[0, late_prompt : late_prompt + 1]
-            start(zm_copies[0])
+            keep, send = split_rows(late_rows() + other, 1, late_bits[0])
+            zd_keep[...] = keep
+            zd_send[...] = to_int16(send * (STEP_UNIT / 2))
+            start(zd_copies[1])
+
+            late_own[0] = bound_own[0, late_prompt : late_prompt + 1]
             for u in late:
                 first_send(u)
 
-        def late_steps(i):
-            zd_copies[i + 1].wait_recv()
-            zm_copies[i].wait_recv()
-            zm_send[i + 1] = zm_send[i] + zm_recv[i]
-            start(zm_copies[i + 1])
-            own, other = zd_keep[i][...], zd_recv[i][...]
-            selected = jnp.where(jnp.full(own.shape, late_bits[i], jnp.int32) == 1, own, other)
-            for k in range(n >> (i + 1)):
-                zd_sel[i][k] = selected[k : k + 1]
-            if i + 1 < levels - 1:
-                late_split(i + 1, own + other)
-
-    for k in range(1, n, 2):
-        send_cache(k)
-    load_pieces[n - 1].wait()
+        def late_steps():
+            zd_copies[1].wait_recv()
+            own, other = zd_keep[...], to_float(zd_recv[...]) * (2 / STEP_UNIT)
+            selected = jnp.where(jnp.full(own.shape, late_bits[0], jnp.int32) == 1, own, other)
+            for k in range(half):
+                zd_sel[k] = selected[k : k + 1]
+
 
     relays = [
         remote(
@@ -400,8 +400,13 @@
             return jnp.maximum(top, jnp.abs(states[p, :, at]))
 
         top = lax.fori_loop(0, channels // top_width, larger, jnp.zeros((state_n, top_width), jnp.float32), unroll=4)
-        m_send[0, p : p + 1] = jnp.maximum(lane_top([top]) * usable[p], 1e-30)
-    start(m_copies[0])
+        bound_own[0, p : p + 1] = jnp.maximum(lane_top([top]) * usable[p], 1e-30)
+    table[me] = bound_own[0]
+    for s in range(levels):
+        for i in range(1 << s):
+            to = bottom(peers[s], s) + i
+            start(remote(bound_own.at[0], table.at[me], m_ss.at[0], m_rs.at[s], {"seq": to}))
+    send_cache(1)
     for u in plain:
         first_send(u)
 
@@ -412,7 +417,8 @@
     owner = lax.broadcasted_iota(jnp.int32, (heads, flat), 0) // group
     same_head = lax.rem(column, kv_heads) == owner
     column_position = (column // kv_heads) * n + me
-    lane_id = lax.broadcasted_iota(jnp.int32, (heads, 128), 1)
+    note_lane = lax.broadcasted_iota(jnp.int32, (heads, 128), 1)
+    note_lane = note_lane - lax.rem(lax.broadcasted_iota(jnp.int32, (heads, 128), 0), own_heads)
 
     def attend(r):
         chosen, hits, length = pick(r, b, requests, all_prompts, plen, tslot, clen)
@@ -443,26 +449,32 @@
         coded = jnp.round(out * (FULL / peak)).astype(jnp.int32)
         for j in range(n):
             osend[j, r * own_heads : (r + 1) * own_heads] = coded[j * own_heads : (j + 1) * own_heads].astype(jnp.int16)
-        noted = jnp.where(lane_id == r, lse, lse_all[...])
-        lse_all[...] = jnp.where(lane_id == requests + r, peak * (1.0 / FULL), noted)
+        noted = jnp.where(note_lane == r * own_heads, lse, lse_all[...])
+        lse_all[...] = jnp.where(note_lane == (requests + r) * own_heads, peak * (1.0 / FULL), noted)
 
     def attention_begin():
         settle(arrived.at[b, pl.ds(0, n - 1)], cache_rs.at[0])
+        load_piece.wait()
         for copy in relays:
             start(copy)
         for copy in load_attention:
             copy.wait()
         lse_all[...] = jnp.zeros((heads, 128), jnp.float32)
 
-    def attention_end():
-        for j in range(n):
-            lse_send[j] = lse_all[j * own_heads : (j + 1) * own_heads]
-        for k in range(1, n):
-            to = lax.rem(me + k, n)
+    def send_out(ks):
+        for k in ks:
+            to = across(k)
+            lse_send[to] = jnp.sum(lse_all[pl.ds(pl.multiple_of(to * own_heads, own_heads), own_heads)], axis=0, keepdims=True)
             start(remote(lse_send.at[to], lse_recv.at[me], l_ss.at[0], l_rs.at[0], {"seq": to}))
             start(remote(osend.at[to], orecv.at[me], o_ss.at[0], o_rs.at[0], {"seq": to}))
-        lse_recv[me] = lse_send[me]
+
+    def attention_end():
+        send_out(range(n - 2, 0, -2))
+        lse_recv[me] = jnp.sum(lse_all[pl.ds(pl.multiple_of(me * own_heads, own_heads), own_heads)], axis=0, keepdims=True)
         orecv[me] = osend[me]
+
+    def attention_last():
+        send_out(range(n - 1, 0, -2))
 
     load_rates.wait()
 
@@ -471,28 +483,25 @@
             for copy in relays:
                 copy.wait_recv()
         attend(r)
-        if r == requests - 1:
-            attention_end()
-
-    def fold_late(s):
-        if s == levels - 1:
-            zm_copies[s].wait_recv()
-        for u in late:
-            fold(s, u)
 
     events = [(D_TIME + D_GAP * s, functools.partial(fold_steps, s)) for s in range(levels)]
+    events += [(BOUND_TIME + BOUND_GAP * s, functools.partial(fold_bounds, s)) for s in range(levels)]
     events.append((RELAY_TIME, attention_begin))
+    events.append((OUT_TIME, attention_end))
+    events.append((OUT_TIME + OUT_GAP, attention_last))
     events += [(ATTEND_TIME + ATTEND_GAP * r, functools.partial(attend_some, r)) for r in range(requests)]
     for i, u in enumerate(plain):
         for s in range(levels):
-            events.append((FOLD_TIME + FOLD_GAP * i + LEVEL_GAP * s, functools.partial(fold, s, u)))
+            lag = FIRST_LAG + NEXT_LAG * (s - 1) if s else 0.0
+            events.append((FOLD_TIME + FOLD_GAP * i + lag, functools.partial(fold, s, u)))
     if late_units:
         events.append((D_TIME + 0.1, late_begin))
-        for s in range(1, levels):
-            events.append((D_TIME + D_GAP * s + 0.1, functools.partial(late_steps, s - 1)))
-            events.append((LATE_TIME + LATE_GAP * (s - 1), functools.partial(fold_late, s - 1)))
-        last = FOLD_TIME + FOLD_GAP * len(plain) + LAST_GAP
-        events.append((last, functools.partial(fold_late, levels - 1)))
+        events.append((D_TIME + D_GAP + 0.1, late_steps))
+        for i, u in enumerate(late):
+            events.append((LATE_TIME + 0.1 * i, functools.partial(fold, 0, u)))
+            for s in range(1, levels):
+                expected = FOLD_TIME + FOLD_GAP * (len(plain) + i / 2) + LATE_GAP + LAST_GAP * (s - 1)
+                events.append((expected, functools.partial(fold, s, u)))
     for _, event in sorted(events, key=lambda e: e[0]):
         event()
 
@@ -505,17 +514,18 @@
         theirs = pl.ds(lax.rem(b + nb - k, nb) * prompts, prompts)
         settle(handed.at[theirs], hand_rs.at[k - 1])
         settle(handed.at[pl.ds(first, prompts)], hand_ss.at[k - 1])
-    settle(cache_send.at[others], cache_ss.at[0])
+    settle(arrived.at[b, others], cache_ss.at[0])
     settle(lse_send.at[others], l_ss.at[0])
     settle(osend.at[others], o_ss.at[0])
     for s in range(levels):
         settle(q_send[s], q_ss.at[s])
-    for copy in relays + d_copies + m_copies + (zd_copies + zm_copies if late_units else []):
+    settle(table.at[others], m_ss.at[0])
+    for copy in relays + d_copies + (zd_copies if late_units else []):
         copy.wait_send()
 
 
-def finish(dims, plen, tslot, clen, merged, handed, orecv, lse_recv, rates, rstates, dt, inner, gate, s_in, s_out, skip,
-           merged_out, attention_out, nstates_out, mout_out, nstates, mout, attention, sems):
+def finish(dims, plen_hbm, tslot_hbm, clen_hbm, merged, handed, orecv, lse_recv, rates, rstates, dt, inner, gate, s_in, s_out, skip,
+           merged_out, attention_out, nstates_out, mout_out, nstates, mout, attention, plen, tslot, clen, sems, scalar_sems):
     n, nb = dims
     b = lax.axis_index("batch")
     all_prompts = handed.shape[0]
@@ -524,6 +534,10 @@
     chunk = min(512, share_len)
     per_share = share_len // chunk
 
+    scalar_copies = []
+    for i, (src, dst) in enumerate(((plen_hbm, plen), (tslot_hbm, tslot), (clen_hbm, clen))):
+        scalar_copies.append(pltpu.make_async_copy(src, dst, scalar_sems.at[i]))
+        scalar_copies[-1].start()
     copies = []
 
     def out(src, dst, i):
@@ -540,6 +554,19 @@
         spread = jnp.where(eye, jnp.broadcast_to(row, (state_n, state_n)), 0.0)
         return jnp.sum(spread, axis=1, keepdims=True)
 
+    note_lane = lax.broadcasted_iota(jnp.int32, (n, own_heads, 128), 2)
+    note_lane = note_lane - lax.broadcasted_iota(jnp.int32, (n, own_heads, 128), 1)
+    noted = jnp.broadcast_to(lse_recv[...], (n, own_heads, 128))
+    for r in range(requests):
+        lse = jnp.sum(jnp.where(note_lane == r * own_heads, noted, 0.0), axis=2, keepdims=True)
+        unit = jnp.sum(jnp.where(note_lane == (requests + r) * own_heads, noted, 0.0), axis=2, keepdims=True)
+        share = jnp.exp(lse - jnp.max(lse, axis=0, keepdims=True))
+        parts = to_float(orecv[:, r * own_heads : (r + 1) * own_heads])
+        top = jnp.sum(share * unit * parts, axis=0)
+        attention[r] = (top / jnp.sum(share, axis=0)).astype(jnp.bfloat16)
+    out(attention, attention_out, 2)
+    for copy in scalar_copies:
+        copy.wait()
     picks = [pick(r, b, requests, all_prompts, plen, tslot, clen) for r in range(requests)]
     in_all, out_all = s_in[...], s_out[...]
     in_cols = [as_column(in_all[r : r + 1]) for r in range(requests)]
@@ -566,16 +593,6 @@
         mout[:, at] = (read_out * (g / (1.0 + jnp.exp(-g)))).astype(jnp.bfloat16)
     out(mout, mout_out, 1)
 
-    lane3 = lax.broadcasted_iota(jnp.int32, (n, own_heads, 128), 2)
-    noted = lse_recv[...]
-    for r in range(requests):
-        lse = jnp.sum(jnp.where(lane3 == r, noted, 0.0), axis=2, keepdims=True)
-        unit = jnp.sum(jnp.where(lane3 == requests + r, noted, 0.0), axis=2, keepdims=True)
-        share = jnp.exp(lse - jnp.max(lse, axis=0, keepdims=True))
-        parts = to_float(orecv[:, r * own_heads : (r + 1) * own_heads])
-        top = jnp.sum(share * unit * parts, axis=0)
-        attention[r] = (top / jnp.sum(share, axis=0)).astype(jnp.bfloat16)
-    out(attention, attention_out, 2)
     for copy in copies:
         copy.wait()
 
@@ -615,7 +632,6 @@
     late_units = LATE
     f32, bf16, i16 = jnp.float32, jnp.bfloat16, jnp.int16
     vmem = pl.BlockSpec(memory_space=pltpu.VMEM)
-    smem = pl.BlockSpec(memory_space=pltpu.SMEM)
     hbm = pl.BlockSpec(memory_space=pltpu.HBM)
     dma = pltpu.SemaphoreType.DMA
     halves = [n >> (s + 1) for s in range(levels)]
@@ -633,12 +649,11 @@
         pltpu.VMEM((requests, positions, kv_heads, width), bf16),
         pltpu.VMEM((all_prompts, state_n, share), f32),
         pltpu.VMEM((n, requests * own_heads, head_dim), i16),
-        pltpu.VMEM((n, own_heads, 128), f32),
+        pltpu.VMEM((n, 1, 128), f32),
         pltpu.VMEM((state_n, share), f32),
     ) + tuple(pltpu.VMEM(x.shape, x.dtype) for x in through)
     scratch = [
         pltpu.VMEM((nb, n, prompts, rows, kv_heads, width), bf16),
-        pltpu.VMEM((n, prompts, rows, kv_heads, width), bf16),
         pltpu.VMEM((prompts, state_n, channels), f32),
         pltpu.VMEM(block_steps.shape, f32),
         pltpu.VMEM((requests, positions, kv_heads, width), bf16),
@@ -647,13 +662,12 @@
         pltpu.VMEM(decay_rates.shape, f32),
         pltpu.VMEM((n, requests * own_heads, head_dim), i16),
         pltpu.VMEM((heads, 128), f32),
-        pltpu.VMEM((n, own_heads, 128), f32),
+        pltpu.VMEM((n, 1, 128), f32),
         pltpu.SMEM(prompt_lengths.shape, jnp.int32),
         pltpu.SMEM(target_slots.shape, jnp.int32),
         pltpu.SMEM(cache_lengths.shape, jnp.int32),
-        dma((9,)),
+        dma((10,)),
         dma((prompts,)),
-        dma((n,)),
         dma((len(through),)),
     ]
     for _ in range(2):
@@ -663,23 +677,22 @@
     for _ in range(2):
         scratch += [pltpu.VMEM((unit_count, h, state_n, piece), i16) for h in halves]
     scratch += [pltpu.VMEM((unit_count, h, state_n, piece), f32) for h in halves[1:]]
+    scratch += [pltpu.VMEM((n, prompts, 128), f32)]
     scratch += [pltpu.VMEM((levels, prompts, 128), f32)] * 2
     if late_units:
         late_lanes = late_units * piece
-        scratch += [pltpu.VMEM((levels, 1, 128), f32)] * 2
+        scratch += [pltpu.VMEM((2, 1, 128), f32)] * 2
         scratch += [pltpu.VMEM((n, late_lanes), i16)] * 2
         scratch += [pltpu.VMEM((n, 1, late_lanes), f32)]
-        scratch += [pltpu.VMEM((late_units, n, state_n, piece), f32)]
-        for _ in range(2):
-            scratch += [pltpu.VMEM((h, late_lanes), f32) for h in halves[: levels - 1]]
-        scratch += [pltpu.VMEM((h, 1, late_lanes), f32) for h in halves[: levels - 1]]
-        scratch += [pltpu.VMEM((h, late_lanes), f32) for h in halves[: levels - 1]]
-        scratch += [dma((levels,))] * 4
+        scratch += [pltpu.VMEM((n // 2, late_lanes), i16)] * 2
+        scratch += [pltpu.VMEM((n // 2, 1, late_lanes), f32)]
+        scratch += [pltpu.VMEM((n // 2, late_lanes), f32)]
+        scratch += [dma((2,))] * 2
     scratch += [dma((1,))] * 2
     scratch += [dma((max(nb - 1, 1),))] * 2
     scratch += [dma((levels,))] * 2
     scratch += [dma((levels,)), dma((levels, unit_count))]
-    scratch += [dma((levels,))] * 2
+    scratch += [dma((1,)), dma((levels,))]
     scratch += [dma((max(nb - 1, 1),))] * 2
     scratch += [dma((1,))] * 4
     scalars = [
@@ -705,13 +718,15 @@
             jax.ShapeDtypeStruct((requests, state_n, share), f32),
             jax.ShapeDtypeStruct((requests, share), bf16),
         ),
-        in_specs=[smem] * 3 + [vmem] * len(parts),
+        in_specs=[hbm] * 3 + [vmem] * len(parts),
         out_specs=(hbm,) * 4,
         scratch_shapes=[
             pltpu.VMEM((requests, state_n, share), f32),
             pltpu.VMEM((requests, share), bf16),
             pltpu.VMEM((requests, own_heads, head_dim), bf16),
+            *(pltpu.SMEM(x.shape, jnp.int32) for x in scalars),
             dma((3 + chunks,)),
+            dma((3,)),
         ],
         compiler_params=pltpu.CompilerParams(vmem_limit_bytes=16 << 20),
     )(*scalars, *parts)

time: 47.7 us -> 46.6 us (0.977)
  Pallas kernels: 46.9 us -> 45.8 us
    pallas_call x1, Pallas kernels: 44.7 us -> 43.8 us  [local(): pl.pallas_call(functools.partial(exchange, (n, nb, levels, block_len, lat...]
where the time goes in v2:
time: 46.6 us; the launch traced here: 46.5 us
  Pallas kernels  45.8 us (98%)
  between operations  0.64 us (1%)
    pallas_call x1, Pallas kernels, local(): pl.pallas_call(functools.partial(exchange, (n, nb, levels, block_len, lat...  43.8 us
    pallas_call x1, Pallas kernels, local(): pl.pallas_call(functools.partial(finish, (n, nb)), out_shape=(jax.ShapeDt...  2.02 us

profile of v2, /device:TPU:0, one launch (start us, length us, event | category | flops | bytes accessed | tf_op | source)
XLA Modules:
  0.0 46.5 jit_solution(16228263038955883887)
XLA Ops:
  0.6 43.8 %shard_map.192 = (bf16[8,32,8,256]{3,2,1,0:T(8,128)(2,1)S(1)}, f32[8,16,2048]{2,1,0:T(8,128)S(1)}, s16[8,64,128]{2,1,0:T(8,128)(2,1)S(1)}, f32[8,1,128]{2,1,0:T(...) custom-call(s32[8]{0:T(128)} %plen_hbm.1, ...), custom_call_target="tpu_custom_call" | custom-call | tf_op jit(solution)/shard_map/pallas_call | solution.py:702
  44.4 2.0 %shard_map.193 = (bf16[8,32,8,256]{3,2,1,0:T(8,128)(2,1)}, bf16[8,8,128]{2,1,0:T(8,128)(2,1)}, f32[8,16,2048]{2,1,0:T(8,128)}, bf16[8,2048]{1,0:T(8,128)(2,1)}) custom-call(s32[8]{0:T(128)} %plen_hbm.1, s32[8]{0:T(128)} %tslot_hbm.1, s32[8]{0:T(128)} %clen_hbm.1, bf16[8,32,8,256]{3,2,1,0:T(8,128)(2,1)S(1)} %get-tuple-element.20.merged, ...), custom_call_target="tpu_custom_call" | custom-call | tf_op jit(solution)/shard_map/pallas_call | solution.py:713

commit v3 on v2

--- a/solution.py
+++ b/solution.py
@@ -19,7 +19,7 @@
 RELAY_TIME, ATTEND_TIME, ATTEND_GAP = 14.5, 15.5, 0.5
 OUT_TIME, OUT_GAP = 19.5, 0.05
 FOLD_TIME, FOLD_GAP, FIRST_LAG, NEXT_LAG = 8.8, 1.39, 5.5, 5.5
-LATE_TIME, LATE_GAP, LAST_GAP = 16.0, 0.5, 4.0
+LATE_TIME, LATE_GAP, LAST_GAP = 13.0, 0.5, 4.0
 
 
 def to_int16(value):
@@ -78,9 +78,10 @@
     scalar_hbm = take(3)
     cache_hbm, states_hbm, steps_hbm, resident_hbm, token_hbm, queries_hbm, rates_hbm = take(7)
     through_hbm = take(7)
-    merged, handed, orecv, lse_recv, rates_own = take(5)
+    merged, handed, attention, rates_own = take(4)
     through = take(7)
     arrived, states, steps, resident, token, queries, rates, osend, lse_all, lse_send = take(10)
+    orecv, lse_recv = take(2)
     plen, tslot, clen = scalars = take(3)
     load_sems, state_sems, through_sems = take(3)
     d_send, d_recv, d_sel = take(levels), take(levels), take(levels)
@@ -510,6 +511,16 @@
     others = pl.ds(0, n - 1)
     settle(lse_recv.at[others], l_rs.at[0])
     settle(orecv.at[others], o_rs.at[0])
+    head_lane = lax.broadcasted_iota(jnp.int32, (n, own_heads, 128), 2)
+    head_lane = head_lane - lax.broadcasted_iota(jnp.int32, (n, own_heads, 128), 1)
+    noted = jnp.broadcast_to(lse_recv[...], (n, own_heads, 128))
+    for r in range(requests):
+        lse = jnp.sum(jnp.where(head_lane == r * own_heads, noted, 0.0), axis=2, keepdims=True)
+        unit = jnp.sum(jnp.where(head_lane == (requests + r) * own_heads, noted, 0.0), axis=2, keepdims=True)
+        share = jnp.exp(lse - jnp.max(lse, axis=0, keepdims=True))
+        parts = to_float(orecv[:, r * own_heads : (r + 1) * own_heads])
+        top = jnp.sum(share * unit * parts, axis=0)
+        attention[r] = (top / jnp.sum(share, axis=0)).astype(jnp.bfloat16)
     for k in range(1, nb):
         theirs = pl.ds(lax.rem(b + nb - k, nb) * prompts, prompts)
         settle(handed.at[theirs], hand_rs.at[k - 1])
@@ -524,13 +535,12 @@
         copy.wait_send()
 
 
-def finish(dims, plen_hbm, tslot_hbm, clen_hbm, merged, handed, orecv, lse_recv, rates, rstates, dt, inner, gate, s_in, s_out, skip,
-           merged_out, attention_out, nstates_out, mout_out, nstates, mout, attention, plen, tslot, clen, sems, scalar_sems):
+def finish(dims, plen_hbm, tslot_hbm, clen_hbm, merged, handed, attention, rates, rstates, dt, inner, gate, s_in, s_out, skip,
+           merged_out, attention_out, nstates_out, mout_out, nstates, mout, plen, tslot, clen, sems, scalar_sems):
     n, nb = dims
     b = lax.axis_index("batch")
     all_prompts = handed.shape[0]
     requests, state_n, share_len = rstates.shape
-    own_heads, head_dim = attention.shape[1:]
     chunk = min(512, share_len)
     per_share = share_len // chunk
 
@@ -546,6 +556,7 @@
         copies.append(copy)
 
     out(merged, merged_out, 0)
+    out(attention, attention_out, 2)
     eye = lax.broadcasted_iota(jnp.int32, (state_n, state_n), 0) == lax.broadcasted_iota(
         jnp.int32, (state_n, state_n), 1
     )
@@ -554,23 +565,12 @@
         spread = jnp.where(eye, jnp.broadcast_to(row, (state_n, state_n)), 0.0)
         return jnp.sum(spread, axis=1, keepdims=True)
 
-    note_lane = lax.broadcasted_iota(jnp.int32, (n, own_heads, 128), 2)
-    note_lane = note_lane - lax.broadcasted_iota(jnp.int32, (n, own_heads, 128), 1)
-    noted = jnp.broadcast_to(lse_recv[...], (n, own_heads, 128))
-    for r in range(requests):
-        lse = jnp.sum(jnp.where(note_lane == r * own_heads, noted, 0.0), axis=2, keepdims=True)
-        unit = jnp.sum(jnp.where(note_lane == (requests + r) * own_heads, noted, 0.0), axis=2, keepdims=True)
-        share = jnp.exp(lse - jnp.max(lse, axis=0, keepdims=True))
-        parts = to_float(orecv[:, r * own_heads : (r + 1) * own_heads])
-        top = jnp.sum(share * unit * parts, axis=0)
-        attention[r] = (top / jnp.sum(share, axis=0)).astype(jnp.bfloat16)
-    out(attention, attention_out, 2)
+    in_all, out_all = s_in[...], s_out[...]
+    in_cols = [as_column(in_all[r : r + 1]) for r in range(requests)]
+    out_cols = [as_column(out_all[r : r + 1]) for r in range(requests)]
     for copy in scalar_copies:
         copy.wait()
     picks = [pick(r, b, requests, all_prompts, plen, tslot, clen) for r in range(requests)]
-    in_all, out_all = s_in[...], s_out[...]
-    in_cols = [as_column(in_all[r : r + 1]) for r in range(requests)]
-    out_cols = [as_column(out_all[r : r + 1]) for r in range(requests)]
 
     for c in range(per_share):
         at = pl.ds(c * chunk, chunk)
@@ -648,8 +648,7 @@
     outs = (
         pltpu.VMEM((requests, positions, kv_heads, width), bf16),
         pltpu.VMEM((all_prompts, state_n, share), f32),
-        pltpu.VMEM((n, requests * own_heads, head_dim), i16),
-        pltpu.VMEM((n, 1, 128), f32),
+        pltpu.VMEM((requests, own_heads, head_dim), bf16),
         pltpu.VMEM((state_n, share), f32),
     ) + tuple(pltpu.VMEM(x.shape, x.dtype) for x in through)
     scratch = [
@@ -662,6 +661,8 @@
         pltpu.VMEM(decay_rates.shape, f32),
         pltpu.VMEM((n, requests * own_heads, head_dim), i16),
         pltpu.VMEM((heads, 128), f32),
+        pltpu.VMEM((n, 1, 128), f32),
+        pltpu.VMEM((n, requests * own_heads, head_dim), i16),
         pltpu.VMEM((n, 1, 128), f32),
         pltpu.SMEM(prompt_lengths.shape, jnp.int32),
         pltpu.SMEM(target_slots.shape, jnp.int32),
@@ -723,7 +724,6 @@
         scratch_shapes=[
             pltpu.VMEM((requests, state_n, share), f32),
             pltpu.VMEM((requests, share), bf16),
-            pltpu.VMEM((requests, own_heads, head_dim), bf16),
             *(pltpu.SMEM(x.shape, jnp.int32) for x in scalars),
             dma((3 + chunks,)),
             dma((3,)),

time: 46.6 us -> 46.3 us (level)
  no operation moved by 1% of the time
where the time goes in v3:
time: 46.3 us; the launch traced here: 46.1 us
  Pallas kernels  45.5 us (98%)
  between operations  0.64 us (1%)
    pallas_call x1, Pallas kernels, local(): pl.pallas_call(functools.partial(exchange, (n, nb, levels, block_len, lat...  43.6 us
    pallas_call x1, Pallas kernels, local(): pl.pallas_call(functools.partial(finish, (n, nb)), out_shape=(jax.ShapeDt...  1.9 us

profile of v3, /device:TPU:0, one launch (start us, length us, event | category | flops | bytes accessed | tf_op | source)
XLA Modules:
  0.0 46.1 jit_solution(1475960628158113964)
XLA Ops:
  0.6 43.6 %shard_map.192 = (bf16[8,32,8,256]{3,2,1,0:T(8,128)(2,1)S(1)}, f32[8,16,2048]{2,1,0:T(8,128)S(1)}, bf16[8,8,128]{2,1,0:T(8,128)(2,1)S(1)}, f32[16,2048]{1,0:T(8,...) custom-call(s32[8]{0:T(128)} %plen_hbm.1, ...), custom_call_target="tpu_custom_call" | custom-call | tf_op jit(solution)/shard_map/pallas_call | solution.py:703
  44.2 1.9 %shard_map.193 = (bf16[8,32,8,256]{3,2,1,0:T(8,128)(2,1)}, bf16[8,8,128]{2,1,0:T(8,128)(2,1)}, f32[8,16,2048]{2,1,0:T(8,128)}, bf16[8,2048]{1,0:T(8,128)(2,1)}) custom-call(s32[8]{0:T(128)} %plen_hbm.1, s32[8]{0:T(128)} %tslot_hbm.1, s32[8]{0:T(128)} %clen_hbm.1, bf16[8,32,8,256]{3,2,1,0:T(8,128)(2,1)S(1)} %get-tuple-element.19.merged, ...), custom_call_target="tpu_custom_call" | custom-call | tf_op jit(solution)/shard_map/pallas_call | solution.py:714

commit v4 on v3

--- a/solution.py
+++ b/solution.py
@@ -568,6 +568,13 @@
     in_all, out_all = s_in[...], s_out[...]
     in_cols = [as_column(in_all[r : r + 1]) for r in range(requests)]
     out_cols = [as_column(out_all[r : r + 1]) for r in range(requests)]
+    for c in range(per_share):
+        at = pl.ds(c * chunk, chunk)
+        step_rows = dt[:, at]
+        rate = -rates[:, at]
+        for r in range(requests):
+            nstates[r, :, at] = jnp.exp(rate * step_rows[r : r + 1])
+
     for copy in scalar_copies:
         copy.wait()
     picks = [pick(r, b, requests, all_prompts, plen, tslot, clen) for r in range(requests)]
@@ -577,14 +584,13 @@
         step_rows = dt[:, at]
         x_rows = inner[:, at].astype(jnp.float32)
         g = gate[:, at].astype(jnp.float32)
-        rate = -rates[:, at]
         push_rows = step_rows * x_rows
         out_rows = []
         for r in range(requests):
             chosen, hits, _ = picks[r]
             fresh = jnp.full((state_n, chunk), hits, jnp.int32) > 0
             begin = jnp.where(fresh, handed[chosen, :, at], rstates[r, :, at])
-            after = jnp.exp(rate * step_rows[r : r + 1]) * begin
+            after = nstates[r, :, at] * begin
             after = after + push_rows[r : r + 1] * in_cols[r]
             nstates[r, :, at] = after
             out_rows.append(jnp.sum(out_cols[r] * after, axis=0, keepdims=True))

time: 46.3 us -> 46.2 us (level)
  no operation moved by 1% of the time
where the time goes in v4:
time: 46.2 us; the launch traced here: 46.1 us
  Pallas kernels  45.4 us (98%)
  between operations  0.64 us (1%)
    pallas_call x1, Pallas kernels, local(): pl.pallas_call(functools.partial(exchange, (n, nb, levels, block_len, lat...  43.6 us
    pallas_call x1, Pallas kernels, local(): pl.pallas_call(functools.partial(finish, (n, nb)), out_shape=(jax.ShapeDt...  1.84 us

profile of v4, /device:TPU:0, one launch (start us, length us, event | category | flops | bytes accessed | tf_op | source)
XLA Modules:
  0.0 46.1 jit_solution(2320859299030945250)
XLA Ops:
  0.6 43.6 %shard_map.192 = (bf16[8,32,8,256]{3,2,1,0:T(8,128)(2,1)S(1)}, f32[8,16,2048]{2,1,0:T(8,128)S(1)}, bf16[8,8,128]{2,1,0:T(8,128)(2,1)S(1)}, f32[16,2048]{1,0:T(8,...) custom-call(s32[8]{0:T(128)} %plen_hbm.1, ...), custom_call_target="tpu_custom_call" | custom-call | tf_op jit(solution)/shard_map/pallas_call | solution.py:709
  44.2 1.8 %shard_map.193 = (bf16[8,32,8,256]{3,2,1,0:T(8,128)(2,1)}, bf16[8,8,128]{2,1,0:T(8,128)(2,1)}, f32[8,16,2048]{2,1,0:T(8,128)}, bf16[8,2048]{1,0:T(8,128)(2,1)}) custom-call(s32[8]{0:T(128)} %plen_hbm.1, s32[8]{0:T(128)} %tslot_hbm.1, s32[8]{0:T(128)} %clen_hbm.1, bf16[8,32,8,256]{3,2,1,0:T(8,128)(2,1)S(1)} %get-tuple-element.19.merged, ...), custom_call_target="tpu_custom_call" | custom-call | tf_op jit(solution)/shard_map/pallas_call | solution.py:720
